TPU v7x, 32 devices: a whole 2x2x4 slice. The times are simulated.
32 devices in a mesh: section: 2 (over x), dp: 16 (over z, y, core).
Axes of the slice: x: 2, y: 2, z: 4, core: 2. Of those that a mesh axis runs over, the one named last changes fastest.
Arguments:
- activations: bfloat16 [2, 8, 768, 5376], P('section', None, 'dp'), may hold values from -6 to 6
- loss_grads: bfloat16 [8, 768, 5376], P(None, 'dp'), may hold values from -6 to 6
- adapter_in: bfloat16 [2, 5376, 64], P('section'), may hold values from -0.078125 to 0.078125
- adapter_out: bfloat16 [2, 64, 5376], P('section'), may hold values from -0.75 to 0.75
- first_moment: float32 [2, 16, 86016], P('section', 'dp'), may hold values from -0.4 to 0.4
- second_moment: float32 [2, 16, 86016], P('section', 'dp'), may hold values from 0.0001 to 0.01
- old_owner: int32 [2, 8], P('section'), may hold values from 0 to 15, as said below
- new_owner: int32 [2, 16], P('section'), may hold values from 0 to 15, each once within a row
- plan: int32 [8], replicated, may hold values from 0 to 7, each once
Outputs:
- input_grads: bfloat16 [2, 8, 768, 5376], P('section', None, 'dp')
- adam_update: float32 [2, 16, 43008], P('section', 'dp')
- first_new: float32 [2, 16, 43008], P('section', 'dp')
- second_new: float32 [2, 16, 43008], P('section', 'dp')
Inputs may be any that keep to these rules, and one draw needn't show every extreme that they name: `old_owner`: the entries of one section's row are distinct.
All inputs are finite; a program needn't handle non-finite values.
Results may differ from a plain program's by a relative error of at most 0.025.
Values may be sent and summed in bfloat16 or wider, within the bound.
A program may use at most 64 MiB of HBM per device.

v0:
```python
import functools
import math

import jax
import jax.numpy as jnp
from jax import lax
from jax.experimental import pallas as pl
from jax.experimental.pallas import tpu as pltpu
from jax.sharding import PartitionSpec as P

beta_one = 0.9
beta_two = 0.95
adam_eps = 1e-08
adam_step = 1000.0
loss_scale = 4096.0
MESH = pl.DeviceIdType.MESH
VMEM = pl.BlockSpec(memory_space=pltpu.VMEM)
SMEM = pl.BlockSpec(memory_space=pltpu.SMEM)
ANY = pl.BlockSpec(memory_space=pl.ANY)


def nt_dot(left, right):
    return lax.dot_general(left, right, (((1,), (1,)), ((), ())), preferred_element_type=jnp.float32)


def column_width(width):
    return 128 * max(d for d in range(1, 8) if (width // 128) % d == 0)


def greet(n, me, extra):
    barrier = pltpu.get_barrier_semaphore()

    @pl.loop(1, n)
    def _(d):
        pl.semaphore_signal(barrier, inc=1, device_id={"dp": lax.rem(me + d, n)}, device_id_type=MESH)

    if extra is not None:
        pl.semaphore_signal(barrier, inc=1, device_id={"section": extra}, device_id_type=MESH)
    pl.semaphore_wait(barrier, n - 1 + (extra is not None))


def relay_kernel(
    n, block_rows, new_ref, old_ref, x_hbm, l_hbm, win_ref, wout_ref, m_ref, v_ref,
    p_up_ref, w_ref, p_ref, total_ref, first_ref, second_ref,
    order, x_buf, l_buf, p_buf, pieces, spread, chosen, got, gin, gout, turn,
    blocks, outbox, near, summed, mid, far,
    x_sem, l_sem, w_send, w_recv, f_send, f_recv, p_send, p_recv, a_send, a_recv, b_send, b_recv, own_sem,
    s1, r1, s2, r2, s3, r3,
):
    me = lax.axis_index("dp")
    section = lax.axis_index("section")
    other = 1 - section
    core = lax.rem(me, 2)
    sibling = me + 1 - 2 * core
    chip = me // 2
    chips = n // 2
    rank, width = win_ref.shape
    cw = column_width(width)
    chunks = width // cw
    loads = []
    for c in range(chunks):
        cols = pl.ds(c * cw, cw)
        for src, dst, sem in ((x_hbm, x_buf, x_sem), (l_hbm, l_buf, l_sem)):
            load = pltpu.make_async_copy(src.at[:, cols], dst.at[:, cols], sem.at[c])
            load.start()
            loads.append(load)
    barrier = pltpu.get_barrier_semaphore()

    @pl.loop(1, n)
    def _(d):
        pl.semaphore_signal(barrier, inc=1, device_id={"dp": lax.rem(me + d, n)}, device_id_type=MESH)

    pl.semaphore_signal(barrier, inc=1, device_id={"section": other}, device_id_type=MESH)
    part = block_rows // n
    slab = pieces.shape[2] // 2
    filler = [jnp.zeros((slab - part, 128), jnp.float32)] if slab > part else []
    for t in range(n):
        for h in range(2):
            start = h * block_rows + t * part
            pieces[t, h] = jnp.concatenate(
                [m_ref[start : start + part, :]] + filler + [v_ref[start : start + part, :]] + filler, axis=0
            ).astype(jnp.bfloat16)
    pl.semaphore_wait(barrier, n)
    half = rank // 2
    mine = pl.ds(pl.multiple_of(core * half, half), half)
    theirs = pl.ds(pl.multiple_of((1 - core) * half, half), half)
    w_copy = pltpu.make_async_remote_copy(
        win_ref.at[mine], w_ref.at[mine], w_send, w_recv, device_id={"section": other}, device_id_type=MESH
    )
    w_copy.start()

    def spread_copy(d):
        peer = lax.rem(me + d, n)
        return pltpu.make_async_remote_copy(
            pieces.at[peer], spread.at[me], a_send.at[d], a_recv.at[d],
            device_id={"dp": peer}, device_id_type=MESH,
        )

    def spread_arrival(d):
        peer = lax.rem(me + n - d, n)
        return pltpu.make_async_remote_copy(
            pieces.at[peer], spread.at[peer], a_send.at[d], a_recv.at[d],
            device_id={"dp": peer}, device_id_type=MESH,
        )

    def gather_copy(d):
        peer = lax.rem(me + d, n)
        return pltpu.make_async_remote_copy(
            chosen.at[peer], got.at[me], b_send.at[d], b_recv.at[d],
            device_id={"dp": peer}, device_id_type=MESH,
        )

    def gather_arrival(d):
        peer = lax.rem(me + n - d, n)
        return pltpu.make_async_remote_copy(
            chosen.at[peer], got.at[peer], b_send.at[d], b_recv.at[d],
            device_id={"dp": peer}, device_id_type=MESH,
        )

    @pl.loop(1, n)
    def _(d):
        spread_copy(d).start()

    own = pltpu.make_async_copy(pieces.at[me], spread.at[me], own_sem.at[0])
    own.start()
    owners = [new_ref[c] for c in range(n)]
    for t in range(n):
        block = jnp.int32(0)
        for c in range(1, n):
            block = jnp.where(owners[c] == t, c, block)
        order[t] = block

    rows = x_buf.shape[0]
    pre = jnp.zeros((rows, rank), jnp.float32)
    act = jnp.zeros((rows, rank), jnp.float32)
    for c in range(chunks):
        cols = pl.ds(c * cw, cw)
        loads[2 * c].wait()
        loads[2 * c + 1].wait()
        pre = pre + nt_dot(x_buf[:, cols], win_ref[:, cols])
        act = act + nt_dot(l_buf[:, cols], wout_ref[:, cols])
    slope = silu_slope(pre)
    p_buf[...] = (act * slope).astype(jnp.bfloat16)
    p_copy = pltpu.make_async_remote_copy(
        p_buf, p_up_ref, p_send, p_recv, device_id={"section": other}, device_id_type=MESH
    )
    p_copy.start()
    hidden_t = jax.nn.silu(pre).T.astype(jnp.bfloat16)
    w_copy.wait_recv()
    forward = pltpu.make_async_remote_copy(
        w_ref.at[mine], w_ref.at[mine], f_send, f_recv, device_id={"dp": sibling}, device_id_type=MESH
    )
    forward.start()
    pltpu.make_async_remote_copy(
        w_ref.at[theirs], w_ref.at[theirs], f_send, f_recv, device_id={"dp": sibling}, device_id_type=MESH
    ).wait_recv()
    p_copy.wait_recv()
    p_in = jnp.where(section == 0, p_up_ref[...].astype(jnp.float32), 0.0).astype(jnp.bfloat16)
    act = jnp.zeros((rows, rank), jnp.float32)
    for c in range(chunks):
        cols = pl.ds(c * cw, cw)
        incoming = (
            l_buf[:, cols].astype(jnp.float32)
            + jnp.dot(p_in, w_ref[:, cols], preferred_element_type=jnp.float32)
        ).astype(jnp.bfloat16)
        act = act + nt_dot(incoming, wout_ref[:, cols])
        gout[:, cols] = jnp.dot(hidden_t, incoming, preferred_element_type=jnp.float32)
    grad = act * slope
    p_ref[...] = grad.astype(jnp.bfloat16)
    p_t = grad.T.astype(jnp.bfloat16)
    own.wait()

    @pl.loop(1, n)
    def _(d):
        spread_arrival(d).wait_recv()

    for t in range(n):
        block = order[t]
        chosen[t] = spread[old_ref[block // 2], lax.rem(block, 2)]

    @pl.loop(1, n)
    def _(d):
        gather_copy(d).start()

    keep = pltpu.make_async_copy(chosen.at[me], got.at[me], own_sem.at[1])
    keep.start()
    for c in range(chunks):
        cols = pl.ds(c * cw, cw)
        gin[cols, :] = jnp.dot(p_t, x_buf[:, cols], preferred_element_type=jnp.float32).T
    tiles = width // 128
    lines = block_rows // tiles
    for b in range(chips):
        start = b * block_rows * 2
        low = gin[pl.ds(start, block_rows, stride=2), :]
        high = gin[pl.ds(start + 1, block_rows, stride=2), :]
        blocks[b] = jnp.concatenate([low, high], axis=1).astype(jnp.bfloat16)
    for b in range(chips):
        for t in range(tiles):
            turn[pl.ds(t, lines, stride=tiles), :] = gout[b * lines : (b + 1) * lines, t * 128 : (t + 1) * 128]
        blocks[chips + b] = turn[...].astype(jnp.bfloat16)

    pairs = chips // 2
    lane = lax.rem(chip, 2)
    pair = chip // 2

    def near_copy(to):
        return pltpu.make_async_remote_copy(
            outbox.at[to], near.at[to], s1.at[to], r1.at[to], device_id={"dp": sibling}, device_id_type=MESH
        )

    def mid_copy(at):
        return pltpu.make_async_remote_copy(
            summed.at[at * 2 + 1 - lane], mid.at[at], s3.at[at], r3.at[at],
            device_id={"dp": (pair * 2 + 1 - lane) * 2 + core}, device_id_type=MESH,
        )

    def far_copy(d):
        to = lax.rem(pair + d, pairs) * 2 + lane
        return pltpu.make_async_remote_copy(
            summed.at[to], far.at[d], s2.at[d], r2.at[d],
            device_id={"dp": to * 2 + core}, device_id_type=MESH,
        )

    for side in (1 - lane, lane):

        @pl.loop(1, pairs + 1)
        def _(step):
            to = lax.rem(pair + step, pairs) * 2 + side
            outbox[to] = blocks[order[to * 2 + 1 - core]]
            near_copy(to).start()

    @pl.loop(1, pairs + 1)
    def _(step):
        at = lax.rem(pair + step, pairs)
        to = at * 2 + 1 - lane
        near_copy(to).wait_recv()
        summed[to] = (
            blocks[order[to * 2 + core]].astype(jnp.float32) + near[to].astype(jnp.float32)
        ).astype(jnp.bfloat16)
        mid_copy(at).start()

    @pl.loop(1, pairs)
    def _(d):
        at = lax.rem(pair + d, pairs)
        to = at * 2 + lane
        near_copy(to).wait_recv()
        mid_copy(at).wait_recv()
        summed[to] = (
            blocks[order[to * 2 + core]].astype(jnp.float32)
            + near[to].astype(jnp.float32)
            + mid[at].astype(jnp.float32)
        ).astype(jnp.bfloat16)
        far_copy(d).start()

    near_copy(chip).wait_recv()
    mid_copy(pair).wait_recv()
    total_ref[...] = (
        blocks[order[me]].astype(jnp.float32) + near[chip].astype(jnp.float32) + mid[pair].astype(jnp.float32)
    )
    keep.wait()

    @pl.loop(1, n)
    def _(d):
        gather_arrival(d).wait_recv()

    for t in range(n):
        place = pl.ds(t * part, part)
        held = got[t].astype(jnp.float32)
        first_ref[place, :] = held[:part, :]
        second_ref[place, :] = held[slab : slab + part, :]

    @pl.loop(1, pairs)
    def _(d):
        far_copy(d).wait_recv()
        total_ref[...] += far[d].astype(jnp.float32)

    w_copy.wait_send()
    p_copy.wait_send()
    forward.wait_send()

    @pl.loop(1, n)
    def _(d):
        spread_copy(d).wait_send()
        gather_copy(d).wait_send()

    @pl.loop(0, chips)
    def _(d):
        near_copy(d).wait_send()

    @pl.loop(0, pairs)
    def _(d):
        mid_copy(d).wait_send()

    @pl.loop(1, pairs)
    def _(d):
        far_copy(d).wait_send()


def relay(n, new_owner, old_owner, x, loss, win, wout, first, second):
    rows, width = x.shape
    rank = win.shape[0]
    chunks = width // column_width(width)
    block_rows = first.shape[0] // 2
    slab = -(-(block_rows // n) // 8) * 8
    dma = pltpu.SemaphoreType.DMA
    bf16, f32 = jnp.bfloat16, jnp.float32
    group = pltpu.VMEM((n // 2, block_rows, 128), bf16)
    fewer = pltpu.VMEM((n // 4, block_rows, 128), bf16)
    lines = jax.ShapeDtypeStruct((block_rows, 128), f32)
    return pl.pallas_call(
        functools.partial(relay_kernel, n, block_rows),
        out_shape=(
            jax.ShapeDtypeStruct((rows, rank), bf16),
            jax.ShapeDtypeStruct((rank, width), bf16),
            jax.ShapeDtypeStruct((rows, rank), bf16),
            lines, lines, lines,
        ),
        in_specs=[SMEM, SMEM, ANY, ANY, VMEM, VMEM, VMEM, VMEM],
        out_specs=(VMEM,) * 6,
        scratch_shapes=[
            pltpu.SMEM((n,), jnp.int32),
            pltpu.VMEM(x.shape, bf16),
            pltpu.VMEM(x.shape, bf16),
            pltpu.VMEM((rows, rank), bf16),
            pltpu.VMEM((n, 2, 2 * slab, 128), bf16),
            pltpu.VMEM((n, 2, 2 * slab, 128), bf16),
            pltpu.VMEM((n, 2 * slab, 128), bf16),
            pltpu.VMEM((n, 2 * slab, 128), bf16),
            pltpu.VMEM((width, rank), f32),
            pltpu.VMEM((rank, width), f32),
            pltpu.VMEM((block_rows, 128), f32),
            pltpu.VMEM((n, block_rows, 128), bf16),
            group, group, group, fewer, fewer,
            dma((chunks,)), dma((chunks,)), dma, dma, dma, dma, dma, dma,
            dma((n,)), dma((n,)), dma((n,)), dma((n,)), dma((2,)),
            dma((n // 2,)), dma((n // 2,)), dma((n // 4,)), dma((n // 4,)), dma((n // 4,)), dma((n // 4,)),
        ],
        compiler_params=pltpu.CompilerParams(collective_id=0, has_side_effects=True),
        name="relay",
    )(new_owner, old_owner, x, loss, win, wout, first, second)


def emit_kernel(
    plan_ref, l_hbm, p_up_ref, w_up_ref, p_ref, win_ref, total_ref, m_ref, v_ref,
    out_hbm, u_ref, first_ref, second_ref,
    l_buf, o_buf, l_sem, o_sem,
):
    rank, width = win_ref.shape
    micro_count, tok_rows, _ = out_hbm.shape
    cw = column_width(width)
    chunks = width // cw
    loads = []
    for c in range(chunks):
        cols = pl.ds(c * cw, cw)
        loads.append(pltpu.make_async_copy(l_hbm.at[:, cols], l_buf.at[:, cols], l_sem.at[c]))
        loads[-1].start()
    adam(total_ref[...], m_ref[...], v_ref[...], u_ref, first_ref, second_ref)
    is_relayed = lax.axis_index("section") == 0
    p_up = jnp.where(is_relayed, p_up_ref[...].astype(jnp.float32), 0.0).astype(jnp.bfloat16)
    p_now = p_ref[...]
    stores = []
    for c in range(chunks):
        cols = pl.ds(c * cw, cw)
        loads[c].wait()
        incoming = (
            l_buf[:, cols].astype(jnp.float32)
            + jnp.dot(p_up, w_up_ref[:, cols], preferred_element_type=jnp.float32)
        ).astype(jnp.bfloat16)
        o_buf[:, cols] = (
            incoming.astype(jnp.float32) + jnp.dot(p_now, win_ref[:, cols], preferred_element_type=jnp.float32)
        ).astype(jnp.bfloat16)
        for m in range(micro_count):
            store = pltpu.make_async_copy(
                o_buf.at[pl.ds(pl.multiple_of(plan_ref[m] * tok_rows, tok_rows), tok_rows), cols],
                out_hbm.at[m, :, cols],
                o_sem.at[c, m],
            )
            store.start()
            stores.append(store)
    for store in stores:
        store.wait()


def emit(micro_count, plan, loss, p_up, w_up, p_now, win, total, m, v):
    rows, width = loss.shape
    chunks = width // column_width(width)
    dma = pltpu.SemaphoreType.DMA
    lines = jax.ShapeDtypeStruct(m.shape, jnp.float32)
    return pl.pallas_call(
        emit_kernel,
        out_shape=(
            jax.ShapeDtypeStruct((micro_count, rows // micro_count, width), jnp.bfloat16),
            lines, lines, lines,
        ),
        in_specs=[SMEM, ANY] + [VMEM] * 7,
        out_specs=(ANY, VMEM, VMEM, VMEM),
        scratch_shapes=[
            pltpu.VMEM(loss.shape, jnp.bfloat16),
            pltpu.VMEM(loss.shape, jnp.bfloat16),
            dma((chunks,)), dma((chunks, micro_count)),
        ],
        name="emit",
    )(plan, loss, p_up, w_up, p_now, win, total, m, v)


def adam(total, m, v, u_ref, first_ref, second_ref):
    grads = total / loss_scale
    first_next = beta_one * m + (1.0 - beta_one) * grads
    second_next = beta_two * v + (1.0 - beta_two) * grads * grads
    first_ref[...] = first_next
    second_ref[...] = second_next
    u_ref[...] = (
        first_next
        / (1.0 - beta_one**adam_step)
        / (jnp.sqrt(second_next / (1.0 - beta_two**adam_step)) + adam_eps)
    )


def reduce_kernel(
    n, q_ref, m_ref, v_ref, u_ref, first_ref, second_ref,
    near, summed, far, s1, r1, s2, r2,
):
    me = lax.axis_index("dp")
    core = lax.rem(me, 2)
    chip = me // 2
    chips = n // 2
    sibling = me + 1 - 2 * core
    greet(n, me, None)

    def near_copy(d):
        to = lax.rem(chip + d, chips)
        return pltpu.make_async_remote_copy(
            q_ref.at[(1 - core) * chips + to], near.at[to], s1.at[d], r1.at[d],
            device_id={"dp": sibling}, device_id_type=MESH,
        )

    def far_copy(d):
        to = lax.rem(chip + d, chips)
        return pltpu.make_async_remote_copy(
            summed.at[to], far.at[d], s2.at[d], r2.at[d],
            device_id={"dp": to * 2 + core}, device_id_type=MESH,
        )

    @pl.loop(1, chips + 1)
    def _(step):
        near_copy(lax.rem(step, chips)).start()

    @pl.loop(1, chips)
    def _(d):
        to = lax.rem(chip + d, chips)
        near_copy(d).wait_recv()
        summed[to] = (
            q_ref[core * chips + to].astype(jnp.float32) + near[to].astype(jnp.float32)
        ).astype(jnp.bfloat16)
        far_copy(d).start()

    near_copy(0).wait_recv()
    total = q_ref[core * chips + chip].astype(jnp.float32) + near[chip].astype(jnp.float32)
    first_ref[...] = total

    @pl.loop(1, chips)
    def _(d):
        far_copy(d).wait_recv()
        first_ref[...] += far[d].astype(jnp.float32)

    adam(first_ref[...], m_ref[...], v_ref[...], u_ref, first_ref, second_ref)

    @pl.loop(0, chips)
    def _(d):
        near_copy(d).wait_send()

    @pl.loop(1, chips)
    def _(d):
        far_copy(d).wait_send()


def reduce_adam(n, blocks, m, v):
    lines = m.shape
    dma = pltpu.SemaphoreType.DMA
    shape = jax.ShapeDtypeStruct(lines, jnp.float32)
    group = pltpu.VMEM((n // 2,) + lines, jnp.bfloat16)
    return pl.pallas_call(
        functools.partial(reduce_kernel, n),
        out_shape=(shape,) * 3,
        in_specs=[VMEM] * 3,
        out_specs=(VMEM,) * 3,
        scratch_shapes=[group, group, group] + [dma((n // 2,))] * 4,
        compiler_params=pltpu.CompilerParams(collective_id=1, has_side_effects=True),
        name="reduce_adam",
    )(blocks, m, v)


def passed_along(value, axis, steps):
    count = lax.axis_size(axis)
    first, last = (max(0, -steps), min(count, count - steps))
    return lax.ppermute(value, axis, [(source, source + steps) for source in range(first, last)])


def silu_slope(pre_value):
    gate_value = jax.nn.sigmoid(pre_value)
    return gate_value * (1.0 + pre_value * (1.0 - gate_value))


def per_device(
    activations,
    loss_grads,
    adapter_in,
    adapter_out,
    first_moment,
    second_moment,
    old_owner,
    new_owner,
    plan,
):
    sections = lax.axis_size("section")
    section_index = lax.axis_index("section")
    replicas = lax.axis_size("dp")
    my_index = lax.axis_index("dp")
    weight_in = adapter_in[0]
    weight_out = adapter_out[0]
    inputs_all = activations[0]
    micro_count = inputs_all.shape[0]
    tok_rows = inputs_all.shape[1]
    width = inputs_all.shape[2]
    owners_old = old_owner[0]
    owners_new = new_owner[0]
    block_len = first_moment.shape[2] // 2
    replica_ids = jnp.arange(replicas, dtype=jnp.int32)
    new_block = jnp.sum(jnp.where(owners_new == my_index, replica_ids, 0))

    def drain_turn(turn_index, state):
        previous, grad_in, grad_out, emitted = state
        received = passed_along(previous, "section", -1)
        slot = turn_index - (sections - 1 - section_index)
        is_valid = (slot >= 0) & (slot < micro_count)
        clamped = jnp.clip(slot, 0, micro_count - 1)
        micro = lax.dynamic_index_in_dim(plan, clamped, 0, keepdims=False)
        section_input = lax.dynamic_index_in_dim(inputs_all, micro, 0, keepdims=False)
        from_loss = lax.dynamic_index_in_dim(loss_grads, micro, 0, keepdims=False)
        incoming = jnp.where(section_index == sections - 1, from_loss, received)
        pre_value = jnp.dot(section_input, weight_in, preferred_element_type=jnp.float32)
        hidden = jax.nn.silu(pre_value).astype(jnp.bfloat16)
        act_grad = jnp.dot(incoming, weight_out.T, preferred_element_type=jnp.float32)
        pre_grad = (act_grad * silu_slope(pre_value)).astype(jnp.bfloat16)
        input_grad = (
            incoming.astype(jnp.float32)
            + jnp.dot(pre_grad, weight_in.T, preferred_element_type=jnp.float32)
        ).astype(jnp.bfloat16)
        valid_weight = is_valid.astype(jnp.float32)
        grad_in = grad_in + valid_weight * jnp.dot(
            section_input.T, pre_grad, preferred_element_type=jnp.float32
        )
        grad_out = grad_out + valid_weight * jnp.dot(
            hidden.T, incoming, preferred_element_type=jnp.float32
        )
        earlier = lax.dynamic_index_in_dim(emitted, clamped, 0, keepdims=False)
        written = jnp.where(is_valid, input_grad, earlier)
        emitted = lax.dynamic_update_index_in_dim(emitted, written, clamped, 0)
        return (input_grad, grad_in, grad_out, emitted)

    start_state = (
        jnp.zeros((tok_rows, width), jnp.bfloat16),
        jnp.zeros(weight_in.shape, jnp.float32),
        jnp.zeros(weight_out.shape, jnp.float32),
        jnp.zeros((micro_count, tok_rows, width), jnp.bfloat16),
    )
    place_of_block = owners_new % 2 * (replicas // 2) + owners_new // 2
    lines = (block_len // 128, 128)
    if sections == 2 and replicas % 4 == 0 and block_len % (128 * replicas) == 0:
        rows = micro_count * tok_rows
        flat_inputs = inputs_all.reshape(rows, width)
        flat_loss = loss_grads.reshape(rows, width)
        turned_in = weight_in.T
        row_lines = (2 * block_len // 128, 128)
        p_up, w_up, p_now, total, first_old, second_old = relay(
            replicas, owners_new, owners_old, flat_inputs, flat_loss, turned_in, weight_out,
            first_moment.reshape(row_lines), second_moment.reshape(row_lines),
        )
        emitted, update, first_next, second_next = emit(
            micro_count, plan, flat_loss, p_up, w_up, p_now, turned_in, total, first_old, second_old
        )
        shape = (1, 1, block_len)
        return (emitted[None], update.reshape(shape), first_next.reshape(shape), second_next.reshape(shape))
    last_grad, grad_in, grad_out, emitted = lax.fori_loop(
        0, micro_count + sections - 1, drain_turn, start_state
    )
    partial_value = jnp.concatenate([grad_in.reshape(-1), grad_out.reshape(-1)])
    block_at = jnp.sum(
        jnp.where(place_of_block[None, :] == replica_ids[:, None], replica_ids[None, :], 0), axis=1
    )
    blocks = jnp.take(partial_value.astype(jnp.bfloat16).reshape((replicas,) + lines), block_at, axis=0)
    old_count = owners_old.shape[0]
    piece_len = 2 * block_len // replicas
    first_pieces = first_moment[0, 0].reshape(replicas, piece_len)
    second_pieces = second_moment[0, 0].reshape(replicas, piece_len)
    first_spread = lax.all_to_all(first_pieces, "dp", split_axis=0, concat_axis=0, tiled=True)
    second_spread = lax.all_to_all(second_pieces, "dp", split_axis=0, concat_axis=0, tiled=True)
    first_held = jnp.take(first_spread, owners_old, axis=0)
    second_held = jnp.take(second_spread, owners_old, axis=0)
    my_half = my_index // old_count
    targets = owners_new.reshape(-1, 2)
    target_of_block = jnp.where(my_half == 0, targets[:, 0], targets[:, 1])
    picker = (target_of_block[None, :] == replica_ids[:, None]).astype(jnp.float32)
    first_out = jnp.dot(picker, first_held, precision=lax.Precision.HIGHEST)
    second_out = jnp.dot(picker, second_held, precision=lax.Precision.HIGHEST)
    first_got = lax.all_to_all(first_out, "dp", split_axis=0, concat_axis=0, tiled=True)
    second_got = lax.all_to_all(second_out, "dp", split_axis=0, concat_axis=0, tiled=True)
    half_start = new_block % 2 * old_count
    first_mine = lax.dynamic_slice_in_dim(first_got, half_start, old_count, 0).reshape(-1)
    second_mine = lax.dynamic_slice_in_dim(second_got, half_start, old_count, 0).reshape(-1)
    update, first_next, second_next = reduce_adam(
        replicas, blocks, first_mine.reshape(lines), second_mine.reshape(lines)
    )
    shape = (1, 1, block_len)
    return (emitted[None], update.reshape(shape), first_next.reshape(shape), second_next.reshape(shape))


def solution(mesh):
    placed = (
        P("section", None, "dp", None),
        P(None, "dp", None),
        P("section", None, None),
        P("section", None, None),
        P("section", "dp", None),
        P("section", "dp", None),
        P("section", None),
        P("section", None),
        P(),
    )
    return jax.shard_map(
        per_device,
        mesh=mesh,
        in_specs=placed,
        out_specs=(
            P("section", None, "dp", None),
            P("section", "dp", None),
            P("section", "dp", None),
            P("section", "dp", None),
        ),
        check_vma=False,
    )
```

profile of v0, /device:TPU:0, one launch (start us, length us, event | category | flops | bytes accessed | tf_op | source)
XLA Modules:
  0.0 49.0 jit_solution(10999001920644191439)
XLA Ops:
  0.6 40.7 %relay.1 = (bf16[384,64]{1,0:T(8,128)(2,1)}, bf16[64,5376]{1,0:T(8,128)(2,1)}, bf16[384,64]{1,0:T(8,128)(2,1)}, f32[336,128]{1,0:T(8,128)}, f32[336,128]{1,0:T(8,128)}, /*index=5*/f32[336,128]{1,0:T(8,128)}) custom-call(s32[16]{0:T(128)} %bitcast.22, s32[8]{0:T(128)} %bitcast.23, bf16[384,5376]{1,0:T(8,128)(2,1)} %bitcast.16, bf16[384,5376]{1,0:T(8,128)(2,1)} %bitcast.14, ...), custom_call_target="tpu_custom_call" | custom-call | tf_op jit(solution)/shard_map/relay/pallas_call | solution.py:310
  41.4 7.7 %emit.1 = (bf16[8,48,5376]{2,1,0:T(8,128)(2,1)}, f32[336,128]{1,0:T(8,128)}, f32[336,128]{1,0:T(8,128)}, f32[336,128]{1,0:T(8,128)}) custom-call(s32[8]{0:T(128)} %plan_ref.1, bf16[384,5376]{1,0:T(8,128)(2,1)} %bitcast.15, bf16[384,64]{1,0:T(8,128)(2,1)} %get-tuple-element.14.p_up_ref, bf16[64,5376]{1,0:T(8,128)(2,1)} %get-tuple-element.15.w_up_ref, ...), custom_call_target="tpu_custom_call" | custom-call | tf_op jit(solution)/shard_map/emit/pallas_call | solution.py:389
where the time goes:
time: 49.2 us; the launch traced here: 49 us
  Pallas kernels  48.4 us (98%)
  between operations  0.64 us (1%)
    pallas_call x1, Pallas kernels, relay(): pl.pallas_call(functools.partial(relay_kernel, n, block_rows), out_shape=...  40.7 us
    pallas_call x1, Pallas kernels, emit(): pl.pallas_call(emit_kernel, out_shape=(jax.ShapeDtypeStruct((micro_count,...  7.68 us

commit v1 on v0

v1 whole, which is shorter than its diff:
```python
import functools
import math

import jax
import jax.numpy as jnp
from jax import lax
from jax.experimental import pallas as pl
from jax.experimental.pallas import tpu as pltpu
from jax.sharding import PartitionSpec as P

beta_one = 0.9
beta_two = 0.95
adam_eps = 1e-08
adam_step = 1000.0
loss_scale = 4096.0
MESH = pl.DeviceIdType.MESH
VMEM = pl.BlockSpec(memory_space=pltpu.VMEM)
SMEM = pl.BlockSpec(memory_space=pltpu.SMEM)
ANY = pl.BlockSpec(memory_space=pl.ANY)
HBM = pl.BlockSpec(memory_space=pltpu.HBM)


def nt_dot(left, right):
    return lax.dot_general(left, right, (((1,), (1,)), ((), ())), preferred_element_type=jnp.float32)


def column_width(width):
    return 128 * max(d for d in range(1, 8) if (width // 128) % d == 0)


def greet(n, me, extra):
    barrier = pltpu.get_barrier_semaphore()

    @pl.loop(1, n)
    def _(d):
        pl.semaphore_signal(barrier, inc=1, device_id={"dp": lax.rem(me + d, n)}, device_id_type=MESH)

    if extra is not None:
        pl.semaphore_signal(barrier, inc=1, device_id={"section": extra}, device_id_type=MESH)
    pl.semaphore_wait(barrier, n - 1 + (extra is not None))


def relay_kernel(
    n, block_rows, pad,
    new_hbm, old_hbm, plan_hbm, x_hbm, l_hbm, win_hbm, wout_hbm, m_hbm, v_hbm,
    o_ref, total_ref, first_ref, second_ref,
    new_ref, old_ref, plan_ref, order, x_buf, l_buf, win_buf, wout_buf, m_buf, v_buf, w_ref, mix,
    p_buf, p_up, p_now, pieces, spread, chosen, got, gin, gout, turn, acc,
    blocks, outbox, near, summed, mid, far,
    i_sem, g_sem, x_sem, l_sem, w_send, w_recv, f_send, f_recv, k_send, k_recv, p_send, p_recv,
    a_send, a_recv, b_send, b_recv, own_sem, s1, r1, s2, r2, s3, r3,
):
    me = lax.axis_index("dp")
    section = lax.axis_index("section")
    other = 1 - section
    core = lax.rem(me, 2)
    sibling = me + 1 - 2 * core
    chip = me // 2
    chips = n // 2
    pairs = chips // 2
    lane = lax.rem(chip, 2)
    pair = chip // 2
    across = (pair * 2 + 1 - lane) * 2
    rank, width = win_hbm.shape
    cw = column_width(width)
    chunks = width // cw
    tiles = width // 128
    lines = block_rows // tiles

    barrier = pltpu.get_barrier_semaphore()

    @pl.loop(1, n)
    def _(d):
        pl.semaphore_signal(barrier, inc=1, device_id={"dp": lax.rem(me + d, n)}, device_id_type=MESH)

    pl.semaphore_signal(barrier, inc=1, device_id={"section": other}, device_id_type=MESH)

    def started(src, dst, sem):
        load = pltpu.make_async_copy(src, dst, sem)
        load.start()
        return load

    ints = [
        started(src, dst, i_sem.at[k])
        for k, (src, dst) in enumerate(((new_hbm, new_ref), (old_hbm, old_ref), (plan_hbm, plan_ref)))
    ]
    weights = [
        started(src, dst, g_sem.at[k])
        for k, (src, dst) in enumerate(
            ((win_hbm, win_buf), (m_hbm, m_buf), (v_hbm, v_buf), (wout_hbm, wout_buf))
        )
    ]
    loads = []
    for c in range(chunks):
        cols = pl.ds(c * cw, cw)
        loads.append(started(x_hbm.at[:, :, cols], x_buf.at[:, :, cols], x_sem.at[c]))
        loads.append(started(l_hbm.at[:, :, cols], l_buf.at[:, :, cols], l_sem.at[c]))

    half, quarter = rank // 2, rank // 4

    def rows_of(core_at, lane_at):
        return pl.ds(pl.multiple_of(core_at * half + lane_at * quarter, quarter), quarter)

    parts = (rows_of(core, lane), rows_of(core, 1 - lane))
    their_parts = (rows_of(1 - core, lane), rows_of(1 - core, 1 - lane))

    def w_copy(k):
        return pltpu.make_async_remote_copy(
            win_buf.at[parts[k]], w_ref.at[parts[k]], w_send.at[k], w_recv.at[k],
            device_id={"section": other}, device_id_type=MESH,
        )

    def forward(k):
        return pltpu.make_async_remote_copy(
            w_ref.at[parts[k]], w_ref.at[parts[k]], f_send.at[k], f_recv.at[k],
            device_id={"dp": sibling}, device_id_type=MESH,
        )

    def forwarded(k):
        return pltpu.make_async_remote_copy(
            w_ref.at[their_parts[k]], w_ref.at[their_parts[k]], f_send.at[k], f_recv.at[k],
            device_id={"dp": sibling}, device_id_type=MESH,
        )

    mix_peers = (
        (sibling, rows_of(1 - core, lane)),
        (across + core, rows_of(core, 1 - lane)),
        (across + 1 - core, rows_of(1 - core, 1 - lane)),
    )

    def mix_copy(k):
        return pltpu.make_async_remote_copy(
            mix.at[parts[0]], mix.at[parts[0]], k_send.at[k], k_recv.at[k],
            device_id={"dp": mix_peers[k][0]}, device_id_type=MESH,
        )

    def mix_arrival(k):
        rows = mix_peers[k][1]
        return pltpu.make_async_remote_copy(
            mix.at[rows], mix.at[rows], k_send.at[k], k_recv.at[k],
            device_id={"dp": mix_peers[k][0]}, device_id_type=MESH,
        )

    p_copy = pltpu.make_async_remote_copy(
        p_buf, p_up, p_send, p_recv, device_id={"section": other}, device_id_type=MESH
    )

    def spread_copy(d):
        peer = lax.rem(me + d, n)
        return pltpu.make_async_remote_copy(
            pieces.at[peer], spread.at[me], a_send.at[d], a_recv.at[d],
            device_id={"dp": peer}, device_id_type=MESH,
        )

    def spread_arrival(d):
        peer = lax.rem(me + n - d, n)
        return pltpu.make_async_remote_copy(
            pieces.at[peer], spread.at[peer], a_send.at[d], a_recv.at[d],
            device_id={"dp": peer}, device_id_type=MESH,
        )

    def gather_copy(d):
        peer = lax.rem(me + d, n)
        return pltpu.make_async_remote_copy(
            chosen.at[peer], got.at[me], b_send.at[d], b_recv.at[d],
            device_id={"dp": peer}, device_id_type=MESH,
        )

    def gather_arrival(d):
        peer = lax.rem(me + n - d, n)
        return pltpu.make_async_remote_copy(
            chosen.at[peer], got.at[peer], b_send.at[d], b_recv.at[d],
            device_id={"dp": peer}, device_id_type=MESH,
        )

    def near_copy(to):
        return pltpu.make_async_remote_copy(
            outbox.at[to], near.at[to], s1.at[to], r1.at[to], device_id={"dp": sibling}, device_id_type=MESH
        )

    def mid_copy(at):
        return pltpu.make_async_remote_copy(
            summed.at[at * 2 + 1 - lane], mid.at[at], s3.at[at], r3.at[at],
            device_id={"dp": across + core}, device_id_type=MESH,
        )

    def far_copy(d):
        to = lax.rem(pair + d, pairs) * 2 + lane
        return pltpu.make_async_remote_copy(
            summed.at[to], far.at[d], s2.at[d], r2.at[d],
            device_id={"dp": to * 2 + core}, device_id_type=MESH,
        )

    weights[0].wait()
    pl.semaphore_wait(barrier, n)
    w_copy(0).start()

    part = block_rows // n
    slab = pieces.shape[2] // 2
    filler = [jnp.zeros((slab - part, 128), jnp.float32)] if slab > part else []
    weights[1].wait()
    weights[2].wait()
    for t in range(n):
        for h in range(2):
            start = h * block_rows + t * part
            pieces[t, h] = jnp.concatenate(
                [m_buf[start : start + part, :]] + filler + [v_buf[start : start + part, :]] + filler, axis=0
            ).astype(jnp.bfloat16)

    @pl.loop(1, n)
    def _(d):
        spread_copy(d).start()

    own = started(pieces.at[me], spread.at[me], own_sem.at[0])
    for load in ints:
        load.wait()
    owners = [new_ref[c] for c in range(n)]
    for t in range(n):
        block = jnp.int32(0)
        for c in range(1, n):
            block = jnp.where(owners[c] == t, c, block)
        order[t] = block
    for b in range(chips):
        blocks[b, block_rows:, :] = jnp.zeros((pad, 128), jnp.bfloat16)

    micro_count, tok_rows, _ = x_buf.shape
    rows = micro_count * tok_rows

    def tokens(ref, cols):
        return ref[:, :, cols].reshape(rows, -1)

    pre = jnp.zeros((rows, rank), jnp.float32)
    act = jnp.zeros((rows, rank), jnp.float32)
    weights[3].wait()
    for c in range(chunks):
        cols = pl.ds(c * cw, cw)
        loads[2 * c].wait()
        pre = pre + nt_dot(tokens(x_buf, cols), win_buf[:, cols])
        loads[2 * c + 1].wait()
        act = act + nt_dot(tokens(l_buf, cols), wout_buf[:, cols])
    slope = silu_slope(pre)
    p_buf[...] = (act * slope).astype(jnp.bfloat16).reshape(p_buf.shape)
    p_copy.start()
    w_copy(1).start()
    hidden_t = jax.nn.silu(pre).T.astype(jnp.bfloat16)

    w_copy(0).wait_recv()
    forward(0).start()
    mixed = nt_dot(w_ref[parts[0], :], wout_buf[...])
    mix[parts[0], :] = jnp.concatenate([mixed, jnp.zeros((quarter, 128 - rank), jnp.float32)], axis=1).astype(
        jnp.bfloat16
    )
    for k in range(3):
        mix_copy(k).start()

    for c in range(chunks):
        cols = pl.ds(c * cw, cw)
        gout[:, cols] = jnp.dot(hidden_t, tokens(l_buf, cols), preferred_element_type=jnp.float32)
    for b in range(chips):
        for t in range(tiles):
            turn[pl.ds(t, lines, stride=tiles), :] = gout[b * lines : (b + 1) * lines, t * 128 : (t + 1) * 128]
        blocks[chips + b, :block_rows, :] = turn[...].astype(jnp.bfloat16)

    p_copy.wait_recv()
    p_in = jnp.where(section == 0, p_up[...].astype(jnp.float32), 0.0).astype(jnp.bfloat16)
    p_up[...] = p_in
    p_in = p_in.reshape(rows, rank)
    shared = jnp.dot(hidden_t, p_in, preferred_element_type=jnp.float32)
    shared = jnp.concatenate([shared, jnp.zeros((rank, 128 - rank), jnp.float32)], axis=1)
    for b in range(chips):
        blocks[chips + b, block_rows:, :] = jnp.concatenate(
            [shared[b * lines : (b + 1) * lines, :], jnp.zeros((pad - lines, 128), jnp.float32)], axis=0
        ).astype(jnp.bfloat16)
    for k in range(3):
        mix_arrival(k).wait_recv()
    grad = (act + jnp.dot(p_in, mix[:, :rank], preferred_element_type=jnp.float32)) * slope
    p_now[...] = grad.astype(jnp.bfloat16).reshape(p_now.shape)
    p_t = grad.T.astype(jnp.bfloat16)
    for c in range(chunks):
        cols = pl.ds(c * cw, cw)
        gin[cols, :] = jnp.dot(p_t, tokens(x_buf, cols), preferred_element_type=jnp.float32).T
    for b in range(chips):
        start = b * block_rows * 2
        low = gin[pl.ds(start, block_rows, stride=2), :]
        high = gin[pl.ds(start + 1, block_rows, stride=2), :]
        blocks[b, :block_rows, :] = jnp.concatenate([low, high], axis=1).astype(jnp.bfloat16)

    for side in (1 - lane, lane):

        @pl.loop(0, pairs)
        def _(at):
            to = at * 2 + side
            outbox[to] = blocks[order[to * 2 + 1 - core]]
            near_copy(to).start()

    @pl.loop(0, pairs)
    def _(at):
        to = at * 2 + 1 - lane
        near_copy(to).wait_recv()
        summed[to] = (
            blocks[order[to * 2 + core]].astype(jnp.float32) + near[to].astype(jnp.float32)
        ).astype(jnp.bfloat16)
        mid_copy(at).start()

    own.wait()

    @pl.loop(1, n)
    def _(d):
        spread_arrival(d).wait_recv()

    for t in range(n):
        block = order[t]
        chosen[t] = spread[old_ref[block // 2], lax.rem(block, 2)]

    @pl.loop(1, n)
    def _(d):
        gather_copy(d).start()

    keep = started(chosen.at[me], got.at[me], own_sem.at[1])
    w_copy(1).wait_recv()
    forward(1).start()


    def drained(ref, cols):
        return jnp.concatenate([ref[plan_ref[m], :, cols] for m in range(micro_count)], axis=0)

    p_up_turn, p_now_turn = drained(p_up, slice(None)), drained(p_now, slice(None))
    forwarded(0).wait_recv()
    forwarded(1).wait_recv()

    def emit(c):
        cols = pl.ds(c * cw, cw)
        incoming = (
            drained(l_buf, cols).astype(jnp.float32) + jnp.dot(p_up_turn, w_ref[:, cols], preferred_element_type=jnp.float32)
        ).astype(jnp.bfloat16)
        o_ref[:, cols] = (
            incoming.astype(jnp.float32)
            + jnp.dot(p_now_turn, win_buf[:, cols], preferred_element_type=jnp.float32)
        ).astype(jnp.bfloat16)

    emitted = 0
    for at in range(pairs):
        until = -(-chunks * (at + 1) // pairs)
        for c in range(emitted, until):
            emit(c)
        emitted = until
        to = at * 2 + lane
        near_copy(to).wait_recv()
        mid_copy(at).wait_recv()
        joined = (
            blocks[order[to * 2 + core]].astype(jnp.float32)
            + near[to].astype(jnp.float32)
            + mid[at].astype(jnp.float32)
        )

        @pl.when(pair != at)
        def _():
            summed[to] = joined.astype(jnp.bfloat16)
            far_copy(lax.rem(at - pair + pairs, pairs)).start()

        @pl.when(pair == at)
        def _():
            acc[...] = joined

    keep.wait()

    @pl.loop(1, n)
    def _(d):
        gather_arrival(d).wait_recv()

    for t in range(n):
        place = pl.ds(t * part, part)
        held = got[t].astype(jnp.float32)
        first_ref[place, :] = held[:part, :]
        second_ref[place, :] = held[slab : slab + part, :]

    @pl.loop(1, pairs)
    def _(d):
        far_copy(d).wait_recv()
        acc[...] += far[d].astype(jnp.float32)

    shared = acc[block_rows : block_rows + lines, :rank].astype(jnp.bfloat16)
    for c in range(chunks):
        fix = jnp.dot(shared, w_ref[:, pl.ds(c * cw, cw)], preferred_element_type=jnp.float32)
        for t in range(cw // 128):
            turn[pl.ds(c * (cw // 128) + t, lines, stride=tiles), :] = fix[:, t * 128 : (t + 1) * 128]
    total_ref[...] = acc[:block_rows, :] + turn[...]

    p_copy.wait_send()
    for k in range(2):
        w_copy(k).wait_send()
        forward(k).wait_send()
    for k in range(3):
        mix_copy(k).wait_send()

    @pl.loop(1, n)
    def _(d):
        spread_copy(d).wait_send()
        gather_copy(d).wait_send()

    @pl.loop(0, chips)
    def _(d):
        near_copy(d).wait_send()

    @pl.loop(0, pairs)
    def _(d):
        mid_copy(d).wait_send()

    @pl.loop(1, pairs)
    def _(d):
        far_copy(d).wait_send()


def in_hbm(array):
    return pltpu.with_memory_space_constraint(array, pltpu.HBM)


def relay(n, new_owner, old_owner, plan, x, loss, win, wout, first, second):
    micro_count, tok_rows, width = x.shape
    rows = micro_count * tok_rows
    rank = win.shape[0]
    chunks = width // column_width(width)
    block_rows = first.shape[0] // 2
    slab = -(-(block_rows // n) // 8) * 8
    lines = block_rows * 128 // width
    pad = -(-(block_rows + lines) // 16) * 16 - block_rows
    dma = pltpu.SemaphoreType.DMA
    bf16, f32 = jnp.bfloat16, jnp.float32
    group = pltpu.VMEM((n // 2, block_rows + pad, 128), bf16)
    fewer = pltpu.VMEM((n // 4, block_rows + pad, 128), bf16)
    out_lines = jax.ShapeDtypeStruct((block_rows, 128), f32)
    return pl.pallas_call(
        functools.partial(relay_kernel, n, block_rows, pad),
        out_shape=(jax.ShapeDtypeStruct((rows, width), bf16), out_lines, out_lines, out_lines),
        in_specs=[HBM] * 9,
        out_specs=(VMEM,) * 4,
        scratch_shapes=[
            pltpu.SMEM(new_owner.shape, jnp.int32),
            pltpu.SMEM(old_owner.shape, jnp.int32),
            pltpu.SMEM(plan.shape, jnp.int32),
            pltpu.SMEM((n,), jnp.int32),
            pltpu.VMEM(x.shape, bf16),
            pltpu.VMEM(x.shape, bf16),
            pltpu.VMEM(win.shape, bf16),
            pltpu.VMEM(win.shape, bf16),
            pltpu.VMEM(first.shape, f32),
            pltpu.VMEM(first.shape, f32),
            pltpu.VMEM(win.shape, bf16),
            pltpu.VMEM((rank, 128), bf16),
            pltpu.VMEM((micro_count, tok_rows, rank), bf16),
            pltpu.VMEM((micro_count, tok_rows, rank), bf16),
            pltpu.VMEM((micro_count, tok_rows, rank), bf16),
            pltpu.VMEM((n, 2, 2 * slab, 128), bf16),
            pltpu.VMEM((n, 2, 2 * slab, 128), bf16),
            pltpu.VMEM((n, 2 * slab, 128), bf16),
            pltpu.VMEM((n, 2 * slab, 128), bf16),
            pltpu.VMEM((width, rank), f32),
            pltpu.VMEM((rank, width), f32),
            pltpu.VMEM((block_rows, 128), f32),
            pltpu.VMEM((block_rows + pad, 128), f32),
            pltpu.VMEM((n, block_rows + pad, 128), bf16),
            group, group, group, fewer, fewer,
            dma((3,)), dma((4,)), dma((chunks,)), dma((chunks,)),
            dma((2,)), dma((2,)), dma((2,)), dma((2,)), dma((3,)), dma((3,)), dma, dma,
            dma((n,)), dma((n,)), dma((n,)), dma((n,)), dma((2,)),
            dma((n // 2,)), dma((n // 2,)), dma((n // 4,)), dma((n // 4,)), dma((n // 4,)), dma((n // 4,)),
        ],
        compiler_params=pltpu.CompilerParams(
            collective_id=0, has_side_effects=True, vmem_limit_bytes=44 * 1024 * 1024
        ),
        name="relay",
    )(*map(in_hbm, (new_owner, old_owner, plan, x, loss, win, wout, first, second)))


def finish_kernel(
    o_ref, total_ref, m_ref, v_ref, out_hbm, u_hbm, first_hbm, second_hbm, u_buf, first_buf, second_buf, sem
):
    count = out_hbm.shape[0]
    stores = []
    for m in range(count):
        tok_rows = out_hbm.shape[1]
        store = pltpu.make_async_copy(o_ref.at[pl.ds(m * tok_rows, tok_rows)], out_hbm.at[m], sem.at[m])
        store.start()
        stores.append(store)
    adam(total_ref[...], m_ref[...], v_ref[...], u_buf, first_buf, second_buf)
    for k, (src, dst) in enumerate(((u_buf, u_hbm), (first_buf, first_hbm), (second_buf, second_hbm))):
        store = pltpu.make_async_copy(src, dst, sem.at[count + k])
        store.start()
        stores.append(store)
    for store in stores:
        store.wait()


def finish(micro_count, o, total, m, v):
    rows, width = o.shape
    lines = jax.ShapeDtypeStruct(m.shape, jnp.float32)
    return pl.pallas_call(
        finish_kernel,
        out_shape=(
            jax.ShapeDtypeStruct((micro_count, rows // micro_count, width), jnp.bfloat16),
            lines, lines, lines,
        ),
        in_specs=[VMEM] * 4,
        out_specs=(ANY,) * 4,
        scratch_shapes=[pltpu.VMEM(m.shape, jnp.float32)] * 3 + [pltpu.SemaphoreType.DMA((micro_count + 3,))],
        compiler_params=pltpu.CompilerParams(vmem_limit_bytes=8 * 1024 * 1024),
        name="finish",
    )(o, total, m, v)


def adam(total, m, v, u_ref, first_ref, second_ref):
    grads = total / loss_scale
    first_next = beta_one * m + (1.0 - beta_one) * grads
    second_next = beta_two * v + (1.0 - beta_two) * grads * grads
    first_ref[...] = first_next
    second_ref[...] = second_next
    u_ref[...] = (
        first_next
        / (1.0 - beta_one**adam_step)
        / (jnp.sqrt(second_next / (1.0 - beta_two**adam_step)) + adam_eps)
    )


def reduce_kernel(
    n, q_ref, m_ref, v_ref, u_ref, first_ref, second_ref,
    near, summed, far, s1, r1, s2, r2,
):
    me = lax.axis_index("dp")
    core = lax.rem(me, 2)
    chip = me // 2
    chips = n // 2
    sibling = me + 1 - 2 * core
    greet(n, me, None)

    def near_copy(d):
        to = lax.rem(chip + d, chips)
        return pltpu.make_async_remote_copy(
            q_ref.at[(1 - core) * chips + to], near.at[to], s1.at[d], r1.at[d],
            device_id={"dp": sibling}, device_id_type=MESH,
        )

    def far_copy(d):
        to = lax.rem(chip + d, chips)
        return pltpu.make_async_remote_copy(
            summed.at[to], far.at[d], s2.at[d], r2.at[d],
            device_id={"dp": to * 2 + core}, device_id_type=MESH,
        )

    @pl.loop(1, chips + 1)
    def _(step):
        near_copy(lax.rem(step, chips)).start()

    @pl.loop(1, chips)
    def _(d):
        to = lax.rem(chip + d, chips)
        near_copy(d).wait_recv()
        summed[to] = (
            q_ref[core * chips + to].astype(jnp.float32) + near[to].astype(jnp.float32)
        ).astype(jnp.bfloat16)
        far_copy(d).start()

    near_copy(0).wait_recv()
    total = q_ref[core * chips + chip].astype(jnp.float32) + near[chip].astype(jnp.float32)
    first_ref[...] = total

    @pl.loop(1, chips)
    def _(d):
        far_copy(d).wait_recv()
        first_ref[...] += far[d].astype(jnp.float32)

    adam(first_ref[...], m_ref[...], v_ref[...], u_ref, first_ref, second_ref)

    @pl.loop(0, chips)
    def _(d):
        near_copy(d).wait_send()

    @pl.loop(1, chips)
    def _(d):
        far_copy(d).wait_send()


def reduce_adam(n, blocks, m, v):
    lines = m.shape
    dma = pltpu.SemaphoreType.DMA
    shape = jax.ShapeDtypeStruct(lines, jnp.float32)
    group = pltpu.VMEM((n // 2,) + lines, jnp.bfloat16)
    return pl.pallas_call(
        functools.partial(reduce_kernel, n),
        out_shape=(shape,) * 3,
        in_specs=[VMEM] * 3,
        out_specs=(VMEM,) * 3,
        scratch_shapes=[group, group, group] + [dma((n // 2,))] * 4,
        compiler_params=pltpu.CompilerParams(collective_id=1, has_side_effects=True),
        name="reduce_adam",
    )(blocks, m, v)


def passed_along(value, axis, steps):
    count = lax.axis_size(axis)
    first, last = (max(0, -steps), min(count, count - steps))
    return lax.ppermute(value, axis, [(source, source + steps) for source in range(first, last)])


def silu_slope(pre_value):
    gate_value = jax.nn.sigmoid(pre_value)
    return gate_value * (1.0 + pre_value * (1.0 - gate_value))


def per_device(
    activations,
    loss_grads,
    adapter_in,
    adapter_out,
    first_moment,
    second_moment,
    old_owner,
    new_owner,
    plan,
):
    sections = lax.axis_size("section")
    section_index = lax.axis_index("section")
    replicas = lax.axis_size("dp")
    my_index = lax.axis_index("dp")
    weight_in = adapter_in[0]
    weight_out = adapter_out[0]
    inputs_all = activations[0]
    micro_count = inputs_all.shape[0]
    tok_rows = inputs_all.shape[1]
    width = inputs_all.shape[2]
    owners_old = old_owner[0]
    owners_new = new_owner[0]
    block_len = first_moment.shape[2] // 2
    replica_ids = jnp.arange(replicas, dtype=jnp.int32)
    new_block = jnp.sum(jnp.where(owners_new == my_index, replica_ids, 0))

    def drain_turn(turn_index, state):
        previous, grad_in, grad_out, emitted = state
        received = passed_along(previous, "section", -1)
        slot = turn_index - (sections - 1 - section_index)
        is_valid = (slot >= 0) & (slot < micro_count)
        clamped = jnp.clip(slot, 0, micro_count - 1)
        micro = lax.dynamic_index_in_dim(plan, clamped, 0, keepdims=False)
        section_input = lax.dynamic_index_in_dim(inputs_all, micro, 0, keepdims=False)
        from_loss = lax.dynamic_index_in_dim(loss_grads, micro, 0, keepdims=False)
        incoming = jnp.where(section_index == sections - 1, from_loss, received)
        pre_value = jnp.dot(section_input, weight_in, preferred_element_type=jnp.float32)
        hidden = jax.nn.silu(pre_value).astype(jnp.bfloat16)
        act_grad = jnp.dot(incoming, weight_out.T, preferred_element_type=jnp.float32)
        pre_grad = (act_grad * silu_slope(pre_value)).astype(jnp.bfloat16)
        input_grad = (
            incoming.astype(jnp.float32)
            + jnp.dot(pre_grad, weight_in.T, preferred_element_type=jnp.float32)
        ).astype(jnp.bfloat16)
        valid_weight = is_valid.astype(jnp.float32)
        grad_in = grad_in + valid_weight * jnp.dot(
            section_input.T, pre_grad, preferred_element_type=jnp.float32
        )
        grad_out = grad_out + valid_weight * jnp.dot(
            hidden.T, incoming, preferred_element_type=jnp.float32
        )
        earlier = lax.dynamic_index_in_dim(emitted, clamped, 0, keepdims=False)
        written = jnp.where(is_valid, input_grad, earlier)
        emitted = lax.dynamic_update_index_in_dim(emitted, written, clamped, 0)
        return (input_grad, grad_in, grad_out, emitted)

    start_state = (
        jnp.zeros((tok_rows, width), jnp.bfloat16),
        jnp.zeros(weight_in.shape, jnp.float32),
        jnp.zeros(weight_out.shape, jnp.float32),
        jnp.zeros((micro_count, tok_rows, width), jnp.bfloat16),
    )
    place_of_block = owners_new % 2 * (replicas // 2) + owners_new // 2
    lines = (block_len // 128, 128)
    if sections == 2 and replicas % 4 == 0 and block_len % (128 * replicas) == 0:
        turned_in = weight_in.T
        row_lines = (2 * block_len // 128, 128)
        o, total, first_old, second_old = relay(
            replicas, owners_new, owners_old, plan, inputs_all, loss_grads, turned_in, weight_out,
            first_moment.reshape(row_lines), second_moment.reshape(row_lines),
        )
        emitted, update, first_next, second_next = finish(micro_count, o, total, first_old, second_old)
        shape = (1, 1, block_len)
        return (emitted[None], update.reshape(shape), first_next.reshape(shape), second_next.reshape(shape))
    last_grad, grad_in, grad_out, emitted = lax.fori_loop(
        0, micro_count + sections - 1, drain_turn, start_state
    )
    partial_value = jnp.concatenate([grad_in.reshape(-1), grad_out.reshape(-1)])
    block_at = jnp.sum(
        jnp.where(place_of_block[None, :] == replica_ids[:, None], replica_ids[None, :], 0), axis=1
    )
    blocks = jnp.take(partial_value.astype(jnp.bfloat16).reshape((replicas,) + lines), block_at, axis=0)
    old_count = owners_old.shape[0]
    piece_len = 2 * block_len // replicas
    first_pieces = first_moment[0, 0].reshape(replicas, piece_len)
    second_pieces = second_moment[0, 0].reshape(replicas, piece_len)
    first_spread = lax.all_to_all(first_pieces, "dp", split_axis=0, concat_axis=0, tiled=True)
    second_spread = lax.all_to_all(second_pieces, "dp", split_axis=0, concat_axis=0, tiled=True)
    first_held = jnp.take(first_spread, owners_old, axis=0)
    second_held = jnp.take(second_spread, owners_old, axis=0)
    my_half = my_index // old_count
    targets = owners_new.reshape(-1, 2)
    target_of_block = jnp.where(my_half == 0, targets[:, 0], targets[:, 1])
    picker = (target_of_block[None, :] == replica_ids[:, None]).astype(jnp.float32)
    first_out = jnp.dot(picker, first_held, precision=lax.Precision.HIGHEST)
    second_out = jnp.dot(picker, second_held, precision=lax.Precision.HIGHEST)
    first_got = lax.all_to_all(first_out, "dp", split_axis=0, concat_axis=0, tiled=True)
    second_got = lax.all_to_all(second_out, "dp", split_axis=0, concat_axis=0, tiled=True)
    half_start = new_block % 2 * old_count
    first_mine = lax.dynamic_slice_in_dim(first_got, half_start, old_count, 0).reshape(-1)
    second_mine = lax.dynamic_slice_in_dim(second_got, half_start, old_count, 0).reshape(-1)
    update, first_next, second_next = reduce_adam(
        replicas, blocks, first_mine.reshape(lines), second_mine.reshape(lines)
    )
    shape = (1, 1, block_len)
    return (emitted[None], update.reshape(shape), first_next.reshape(shape), second_next.reshape(shape))


def solution(mesh):
    placed = (
        P("section", None, "dp", None),
        P(None, "dp", None),
        P("section", None, None),
        P("section", None, None),
        P("section", "dp", None),
        P("section", "dp", None),
        P("section", None),
        P("section", None),
        P(),
    )
    return jax.shard_map(
        per_device,
        mesh=mesh,
        in_specs=placed,
        out_specs=(
            P("section", None, "dp", None),
            P("section", "dp", None),
            P("section", "dp", None),
            P("section", "dp", None),
        ),
        check_vma=False,
    )
```

time: 49.2 us -> 41.1 us (0.84)
  the two profiles are of different devices: /device:TPU:0 before, /device:TPU:25 now
where the time goes in v1:
time: 41.1 us; the launch traced here: 40.9 us
  Pallas kernels  40.3 us (98%)
  between operations  0.64 us (2%)
    pallas_call x1, Pallas kernels, relay(): pl.pallas_call(functools.partial(relay_kernel, n, block_rows, pad), out_s...  38.1 us
    pallas_call x1, Pallas kernels, finish(): pl.pallas_call(finish_kernel, out_shape=(jax.ShapeDtypeStruct((micro_coun...  2.24 us

profile of v1, /device:TPU:25, one launch (start us, length us, event | category | flops | bytes accessed | tf_op | source)
XLA Modules:
  0.0 40.9 jit_solution(6290630006378618212)
XLA Ops:
  0.6 38.1 %relay.1 = (bf16[384,5376]{1,0:T(8,128)(2,1)S(1)}, f32[336,128]{1,0:T(8,128)S(1)}, f32[336,128]{1,0:T(8,128)S(1)}, f32[336,128]{1,0:T(8,128)S(1)}) custom-call(s32[16]{0:T(128)} %bitcast.18, s32[8]{0:T(128)} %bitcast.19, s32[8]{0:T(128)} %plan_hbm.1, bf16[8,48,5376]{2,1,0:T(8,128)(2,1)} %bitcast.13, bf16[8,48,5376]{2,1,0:T(8,128)(2,1)} %l_hbm.1, ...), custom_call_target="tpu_custom_call" | custom-call | tf_op jit(solution)/shard_map/relay/pallas_call | solution.py:432
  38.7 2.2 %finish.1 = (bf16[8,48,5376]{2,1,0:T(8,128)(2,1)}, f32[336,128]{1,0:T(8,128)}, f32[336,128]{1,0:T(8,128)}, f32[336,128]{1,0:T(8,128)}) custom-call(bf16[384,5376]{1,0:T(8,128)(2,1)S(1)} %get-tuple-element.12.o_ref, f32[336,128]{1,0:T(8,128)S(1)} %get-tuple-element.13.total_ref, f32[336,128]{1,0:T(8,128)S(1)} %get-tuple-element.14.m_ref, ...), custom_call_target="tpu_custom_call" | custom-call | tf_op jit(solution)/shard_map/finish/pallas_call | solution.py:497

commit v2 on v1

--- a/solution.py
+++ b/solution.py
@@ -44,10 +44,10 @@
     n, block_rows, pad,
     new_hbm, old_hbm, plan_hbm, x_hbm, l_hbm, win_hbm, wout_hbm, m_hbm, v_hbm,
     o_ref, total_ref, first_ref, second_ref,
-    new_ref, old_ref, plan_ref, order, x_buf, l_buf, win_buf, wout_buf, m_buf, v_buf, w_ref, mix,
-    p_buf, p_up, p_now, pieces, spread, chosen, got, gin, gout, turn, acc,
+    new_ref, old_ref, plan_ref, order, x_buf, l_buf, win_buf, wout_buf, m_buf, v_buf, w_ref, mix_out, mix, mix_t, act_buf,
+    p_out, p_got, p_up, p_now, pieces, spread, chosen, got, gin, gout, turn, acc,
     blocks, outbox, near, summed, mid, far,
-    i_sem, g_sem, x_sem, l_sem, w_send, w_recv, f_send, f_recv, k_send, k_recv, p_send, p_recv,
+    i_sem, g_sem, x_sem, l_sem, w_send, w_recv, f_send, f_recv, k_send, k_recv, j_send, j_recv, p_send, p_recv,
     a_send, a_recv, b_send, b_recv, own_sem, s1, r1, s2, r2, s3, r3,
 ):
     me = lax.axis_index("dp")
@@ -73,7 +73,8 @@
     def _(d):
         pl.semaphore_signal(barrier, inc=1, device_id={"dp": lax.rem(me + d, n)}, device_id_type=MESH)
 
-    pl.semaphore_signal(barrier, inc=1, device_id={"section": other}, device_id_type=MESH)
+    for peer in (me, sibling, across + core, across + 1 - core):
+        pl.semaphore_signal(barrier, inc=1, device_id={"section": other, "dp": peer}, device_id_type=MESH)
 
     def started(src, dst, sem):
         load = pltpu.make_async_copy(src, dst, sem)
@@ -87,14 +88,17 @@
     weights = [
         started(src, dst, g_sem.at[k])
         for k, (src, dst) in enumerate(
-            ((win_hbm, win_buf), (m_hbm, m_buf), (v_hbm, v_buf), (wout_hbm, wout_buf))
+            ((m_hbm, m_buf), (v_hbm, v_buf), (win_hbm, win_buf), (wout_hbm, wout_buf))
         )
     ]
+    micro_count, tok_rows, _ = x_buf.shape
+    rows = micro_count * tok_rows
+    edges = [micro_count * k // 8 for k in (0, 4, 6, 8)]
+    spans = [pl.ds(a, b - a) for a, b in zip(edges, edges[1:])]
     loads = []
-    for c in range(chunks):
-        cols = pl.ds(c * cw, cw)
-        loads.append(started(x_hbm.at[:, :, cols], x_buf.at[:, :, cols], x_sem.at[c]))
-        loads.append(started(l_hbm.at[:, :, cols], l_buf.at[:, :, cols], l_sem.at[c]))
+    for g, span in enumerate(spans):
+        loads.append(started(x_hbm.at[span], x_buf.at[span], x_sem.at[g]))
+        loads.append(started(l_hbm.at[span], l_buf.at[span], l_sem.at[g]))
 
     half, quarter = rank // 2, rank // 4
 
@@ -104,9 +108,19 @@
     parts = (rows_of(core, lane), rows_of(core, 1 - lane))
     their_parts = (rows_of(1 - core, lane), rows_of(1 - core, 1 - lane))
 
+    low = pl.ds(0, tiles // 2 * 128)
+    high = pl.ds(tiles // 2 * 128, width - tiles // 2 * 128)
+
+    def lend(src, cols):
+        return pltpu.make_async_remote_copy(
+            src.at[parts[0], cols], w_ref.at[parts[0], low], w_send.at[0], w_recv.at[0],
+            device_id={"section": other}, device_id_type=MESH,
+        )
+
     def w_copy(k):
-        return pltpu.make_async_remote_copy(
-            win_buf.at[parts[k]], w_ref.at[parts[k]], w_send.at[k], w_recv.at[k],
+        spot = (parts[0], high) if k == 2 else (parts[1],)
+        return pltpu.make_async_remote_copy(
+            win_hbm.at[spot], w_ref.at[spot], w_send.at[k], w_recv.at[k],
             device_id={"section": other}, device_id_type=MESH,
         )
 
@@ -122,7 +136,8 @@
             device_id={"dp": sibling}, device_id_type=MESH,
         )
 
-    mix_peers = (
+    group = (
+        (me, rows_of(core, lane)),
         (sibling, rows_of(1 - core, lane)),
         (across + core, rows_of(core, 1 - lane)),
         (across + 1 - core, rows_of(1 - core, 1 - lane)),
@@ -130,76 +145,81 @@
 
     def mix_copy(k):
         return pltpu.make_async_remote_copy(
-            mix.at[parts[0]], mix.at[parts[0]], k_send.at[k], k_recv.at[k],
-            device_id={"dp": mix_peers[k][0]}, device_id_type=MESH,
-        )
-
-    def mix_arrival(k):
-        rows = mix_peers[k][1]
-        return pltpu.make_async_remote_copy(
-            mix.at[rows], mix.at[rows], k_send.at[k], k_recv.at[k],
-            device_id={"dp": mix_peers[k][0]}, device_id_type=MESH,
-        )
-
-    p_copy = pltpu.make_async_remote_copy(
-        p_buf, p_up, p_send, p_recv, device_id={"section": other}, device_id_type=MESH
-    )
+            mix_out, mix.at[parts[0]], k_send, k_recv,
+            device_id={"dp": group[k][0]}, device_id_type=MESH,
+        )
+
+    def mix_t_copy(k):
+        return pltpu.make_async_remote_copy(
+            mix_out, mix_t.at[parts[0]], j_send, j_recv,
+            device_id={"section": other, "dp": group[k][0]}, device_id_type=MESH,
+        )
+
+    def p_copy(k):
+        return pltpu.make_async_remote_copy(
+            p_out.at[k], p_got.at[k], p_send.at[k], p_recv.at[k], device_id={"section": other}, device_id_type=MESH
+        )
 
     def spread_copy(d):
         peer = lax.rem(me + d, n)
         return pltpu.make_async_remote_copy(
-            pieces.at[peer], spread.at[me], a_send.at[d], a_recv.at[d],
+            pieces.at[peer], spread.at[me], a_send, a_recv,
             device_id={"dp": peer}, device_id_type=MESH,
         )
 
-    def spread_arrival(d):
-        peer = lax.rem(me + n - d, n)
-        return pltpu.make_async_remote_copy(
-            pieces.at[peer], spread.at[peer], a_send.at[d], a_recv.at[d],
-            device_id={"dp": peer}, device_id_type=MESH,
+    def spread_all():
+        return pltpu.make_async_remote_copy(
+            pieces.at[pl.ds(0, n - 1)], spread.at[pl.ds(0, n - 1)], a_send, a_recv,
+            device_id={"dp": sibling}, device_id_type=MESH,
         )
 
     def gather_copy(d):
         peer = lax.rem(me + d, n)
         return pltpu.make_async_remote_copy(
-            chosen.at[peer], got.at[me], b_send.at[d], b_recv.at[d],
+            chosen.at[peer], got.at[me], b_send, b_recv,
             device_id={"dp": peer}, device_id_type=MESH,
         )
 
-    def gather_arrival(d):
-        peer = lax.rem(me + n - d, n)
-        return pltpu.make_async_remote_copy(
-            chosen.at[peer], got.at[peer], b_send.at[d], b_recv.at[d],
-            device_id={"dp": peer}, device_id_type=MESH,
+    def gather_all():
+        return pltpu.make_async_remote_copy(
+            chosen.at[pl.ds(0, n - 1)], got.at[pl.ds(0, n - 1)], b_send, b_recv,
+            device_id={"dp": sibling}, device_id_type=MESH,
         )
 
     def near_copy(to):
         return pltpu.make_async_remote_copy(
-            outbox.at[to], near.at[to], s1.at[to], r1.at[to], device_id={"dp": sibling}, device_id_type=MESH
+            outbox.at[to], near.at[to], s1, r1.at[to], device_id={"dp": sibling}, device_id_type=MESH
         )
 
     def mid_copy(at):
         return pltpu.make_async_remote_copy(
-            summed.at[at * 2 + 1 - lane], mid.at[at], s3.at[at], r3.at[at],
+            summed.at[at * 2 + 1 - lane], mid.at[at], s3, r3.at[at],
             device_id={"dp": across + core}, device_id_type=MESH,
         )
 
     def far_copy(d):
         to = lax.rem(pair + d, pairs) * 2 + lane
         return pltpu.make_async_remote_copy(
-            summed.at[to], far.at[d], s2.at[d], r2.at[d],
+            summed.at[to], far.at[d], s2, r2.at[d],
             device_id={"dp": to * 2 + core}, device_id_type=MESH,
         )
 
-    weights[0].wait()
-    pl.semaphore_wait(barrier, n)
-    w_copy(0).start()
+    pl.semaphore_wait(barrier, n + 3)
+
+    @pl.when(section == 0)
+    def _():
+        lend(wout_hbm, high).start()
+
+    @pl.when(section == 1)
+    def _():
+        lend(win_hbm, low).start()
+
 
     part = block_rows // n
     slab = pieces.shape[2] // 2
     filler = [jnp.zeros((slab - part, 128), jnp.float32)] if slab > part else []
+    weights[0].wait()
     weights[1].wait()
-    weights[2].wait()
     for t in range(n):
         for h in range(2):
             start = h * block_rows + t * part
@@ -220,38 +240,58 @@
         for c in range(1, n):
             block = jnp.where(owners[c] == t, c, block)
         order[t] = block
-    for b in range(chips):
+    for b in range(n):
         blocks[b, block_rows:, :] = jnp.zeros((pad, 128), jnp.bfloat16)
 
-    micro_count, tok_rows, _ = x_buf.shape
-    rows = micro_count * tok_rows
 
     def tokens(ref, cols):
         return ref[:, :, cols].reshape(rows, -1)
 
-    pre = jnp.zeros((rows, rank), jnp.float32)
-    act = jnp.zeros((rows, rank), jnp.float32)
+    weights[2].wait()
     weights[3].wait()
-    for c in range(chunks):
-        cols = pl.ds(c * cw, cw)
-        loads[2 * c].wait()
-        pre = pre + nt_dot(tokens(x_buf, cols), win_buf[:, cols])
-        loads[2 * c + 1].wait()
-        act = act + nt_dot(tokens(l_buf, cols), wout_buf[:, cols])
-    slope = silu_slope(pre)
-    p_buf[...] = (act * slope).astype(jnp.bfloat16).reshape(p_buf.shape)
-    p_copy.start()
-    w_copy(1).start()
+    pres, acts, slopes = [], [], []
+    sent = 0
+    for g, span in enumerate(spans):
+        loads[2 * g].wait()
+        loads[2 * g + 1].wait()
+        pres.append(nt_dot(x_buf[span].reshape(-1, width), win_buf[...]))
+        acts.append(nt_dot(l_buf[span].reshape(-1, width), wout_buf[...]))
+        slopes.append(silu_slope(pres[-1]))
+        if 2 * edges[g + 1] >= (sent + 1) * micro_count:
+            grad = jnp.concatenate(acts, axis=0) * jnp.concatenate(slopes, axis=0)
+            top = sent * rows // 2
+            p_out[sent] = jnp.concatenate(
+                [grad[top : top + rows // 4], grad[top + rows // 4 : top + rows // 2]], axis=1
+            ).astype(jnp.bfloat16)
+
+            @pl.when(section == 1)
+            def _():
+                p_copy(sent).start()
+
+            sent += 1
+    pre, act, slope = (jnp.concatenate(parts_of, axis=0) for parts_of in (pres, acts, slopes))
     hidden_t = jax.nn.silu(pre).T.astype(jnp.bfloat16)
-
-    w_copy(0).wait_recv()
-    forward(0).start()
-    mixed = nt_dot(w_ref[parts[0], :], wout_buf[...])
-    mix[parts[0], :] = jnp.concatenate([mixed, jnp.zeros((quarter, 128 - rank), jnp.float32)], axis=1).astype(
-        jnp.bfloat16
-    )
-    for k in range(3):
-        mix_copy(k).start()
+    act_buf[...] = act
+
+    lend(win_hbm, low).wait_recv()
+
+    def mixed(weight, cols):
+        value = nt_dot(w_ref[parts[0], low], weight[:, cols])
+        value = jnp.concatenate([value, jnp.zeros((quarter, 128 - rank), jnp.float32)], axis=1)
+        return value.astype(jnp.bfloat16)
+
+    @pl.when(section == 0)
+    def _():
+        mix_out[...] = mixed(wout_buf, low)
+        mix[parts[0], :] = mix_out[...]
+        for k in range(1, 4):
+            mix_copy(k).start()
+
+    @pl.when(section == 1)
+    def _():
+        mix_out[...] = mixed(win_buf, high)
+        for k in range(4):
+            mix_t_copy(k).start()
 
     for c in range(chunks):
         cols = pl.ds(c * cw, cw)
@@ -261,40 +301,70 @@
             turn[pl.ds(t, lines, stride=tiles), :] = gout[b * lines : (b + 1) * lines, t * 128 : (t + 1) * 128]
         blocks[chips + b, :block_rows, :] = turn[...].astype(jnp.bfloat16)
 
-    p_copy.wait_recv()
-    p_in = jnp.where(section == 0, p_up[...].astype(jnp.float32), 0.0).astype(jnp.bfloat16)
-    p_up[...] = p_in
-    p_in = p_in.reshape(rows, rank)
-    shared = jnp.dot(hidden_t, p_in, preferred_element_type=jnp.float32)
-    shared = jnp.concatenate([shared, jnp.zeros((rank, 128 - rank), jnp.float32)], axis=1)
-    for b in range(chips):
-        blocks[chips + b, block_rows:, :] = jnp.concatenate(
-            [shared[b * lines : (b + 1) * lines, :], jnp.zeros((pad - lines, 128), jnp.float32)], axis=0
-        ).astype(jnp.bfloat16)
-    for k in range(3):
-        mix_arrival(k).wait_recv()
-    grad = (act + jnp.dot(p_in, mix[:, :rank], preferred_element_type=jnp.float32)) * slope
+    @pl.when(section == 1)
+    def _():
+        p_up[...] = jnp.zeros_like(p_up)
+
+    @pl.when(section == 0)
+    def _():
+        p_copy(0).wait_recv()
+        p_copy(1).wait_recv()
+        p_in = jnp.concatenate([p_got[k, :, c : c + rank] for k in range(2) for c in (0, rank)], axis=0)
+        p_up[...] = p_in.reshape(p_up.shape)
+        shared = jnp.dot(hidden_t, p_in, preferred_element_type=jnp.float32)
+        shared = jnp.concatenate([shared, jnp.zeros((rank, 128 - rank), jnp.float32)], axis=1)
+        for b in range(chips):
+            blocks[chips + b, block_rows:, :] = jnp.concatenate(
+                [shared[b * lines : (b + 1) * lines, :], jnp.zeros((pad - lines, 128), jnp.float32)], axis=0
+            ).astype(jnp.bfloat16)
+        pltpu.make_async_remote_copy(
+            mix.at[pl.ds(0, 3 * quarter)], mix.at[pl.ds(0, 3 * quarter)], k_send, k_recv,
+            device_id={"dp": sibling}, device_id_type=MESH,
+        ).wait_recv()
+        pltpu.make_async_remote_copy(
+            mix_t, mix_t, j_send, j_recv, device_id={"section": other}, device_id_type=MESH
+        ).wait_recv()
+        act_buf[...] += jnp.dot(p_in, mix[:, :rank], preferred_element_type=jnp.float32) + nt_dot(
+            p_in, mix_t[:, :rank]
+        )
+
+    w_copy(2).start()
+    w_copy(1).start()
+    grad = act_buf[...] * slope
     p_now[...] = grad.astype(jnp.bfloat16).reshape(p_now.shape)
     p_t = grad.T.astype(jnp.bfloat16)
-    for c in range(chunks):
-        cols = pl.ds(c * cw, cw)
+    groups = math.gcd(tiles, chips)
+    for g in range(groups):
+        cols = pl.ds(g * (width // groups), width // groups)
         gin[cols, :] = jnp.dot(p_t, tokens(x_buf, cols), preferred_element_type=jnp.float32).T
-    for b in range(chips):
-        start = b * block_rows * 2
-        low = gin[pl.ds(start, block_rows, stride=2), :]
-        high = gin[pl.ds(start + 1, block_rows, stride=2), :]
-        blocks[b, :block_rows, :] = jnp.concatenate([low, high], axis=1).astype(jnp.bfloat16)
-
+        for b in range(g * chips // groups, (g + 1) * chips // groups):
+            start = b * block_rows * 2
+            even = gin[pl.ds(start, block_rows, stride=2), :]
+            odd = gin[pl.ds(start + 1, block_rows, stride=2), :]
+            blocks[b, :block_rows, :] = jnp.concatenate([even, odd], axis=1).astype(jnp.bfloat16)
+
+    own.wait()
+
+    spread_all().wait_recv()
+
+    for t in range(n):
+        block = order[t]
+        chosen[t] = spread[old_ref[block // 2], lax.rem(block, 2)]
+
+    @pl.loop(1, n)
+    def _(d):
+        gather_copy(d).start()
+
+    keep = started(chosen.at[me], got.at[me], own_sem.at[1])
+    table = [sorted(range(pairs), key=lambda at, p=p: (-abs(at - p), at)) for p in range(pairs)]
+    turns = [sum(jnp.where(pair == p, table[p][k], 0) for p in range(pairs)) for k in range(pairs)]
     for side in (1 - lane, lane):
-
-        @pl.loop(0, pairs)
-        def _(at):
+        for at in turns:
             to = at * 2 + side
             outbox[to] = blocks[order[to * 2 + 1 - core]]
             near_copy(to).start()
 
-    @pl.loop(0, pairs)
-    def _(at):
+    for at in turns:
         to = at * 2 + 1 - lane
         near_copy(to).wait_recv()
         summed[to] = (
@@ -302,21 +372,8 @@
         ).astype(jnp.bfloat16)
         mid_copy(at).start()
 
-    own.wait()
-
-    @pl.loop(1, n)
-    def _(d):
-        spread_arrival(d).wait_recv()
-
-    for t in range(n):
-        block = order[t]
-        chosen[t] = spread[old_ref[block // 2], lax.rem(block, 2)]
-
-    @pl.loop(1, n)
-    def _(d):
-        gather_copy(d).start()
-
-    keep = started(chosen.at[me], got.at[me], own_sem.at[1])
+    w_copy(2).wait_recv()
+    forward(0).start()
     w_copy(1).wait_recv()
     forward(1).start()
 
@@ -339,8 +396,8 @@
         ).astype(jnp.bfloat16)
 
     emitted = 0
-    for at in range(pairs):
-        until = -(-chunks * (at + 1) // pairs)
+    for step, at in enumerate(turns):
+        until = -(-chunks * (step + 1) // pairs)
         for c in range(emitted, until):
             emit(c)
         emitted = until
@@ -353,20 +410,15 @@
             + mid[at].astype(jnp.float32)
         )
 
-        @pl.when(pair != at)
-        def _():
+        if step < pairs - 1:
             summed[to] = joined.astype(jnp.bfloat16)
             far_copy(lax.rem(at - pair + pairs, pairs)).start()
-
-        @pl.when(pair == at)
-        def _():
+        else:
             acc[...] = joined
 
     keep.wait()
 
-    @pl.loop(1, n)
-    def _(d):
-        gather_arrival(d).wait_recv()
+    gather_all().wait_recv()
 
     for t in range(n):
         place = pl.ds(t * part, part)
@@ -386,29 +438,38 @@
             turn[pl.ds(c * (cw // 128) + t, lines, stride=tiles), :] = fix[:, t * 128 : (t + 1) * 128]
     total_ref[...] = acc[:block_rows, :] + turn[...]
 
-    p_copy.wait_send()
+    lend(win_hbm, low).wait_send()
     for k in range(2):
-        w_copy(k).wait_send()
+        w_copy(k + 1).wait_send()
         forward(k).wait_send()
-    for k in range(3):
-        mix_copy(k).wait_send()
-
-    @pl.loop(1, n)
-    def _(d):
-        spread_copy(d).wait_send()
-        gather_copy(d).wait_send()
-
-    @pl.loop(0, chips)
-    def _(d):
-        near_copy(d).wait_send()
-
-    @pl.loop(0, pairs)
-    def _(d):
-        mid_copy(d).wait_send()
-
-    @pl.loop(1, pairs)
-    def _(d):
-        far_copy(d).wait_send()
+
+    @pl.when(section == 0)
+    def _():
+        pltpu.make_async_remote_copy(
+            mix.at[pl.ds(0, 3 * quarter)], mix.at[pl.ds(0, 3 * quarter)], k_send, k_recv,
+            device_id={"dp": sibling}, device_id_type=MESH,
+        ).wait_send()
+
+    @pl.when(section == 1)
+    def _():
+        p_copy(0).wait_send()
+        p_copy(1).wait_send()
+        pltpu.make_async_remote_copy(
+            mix_t, mix_t, j_send, j_recv, device_id={"section": other}, device_id_type=MESH
+        ).wait_send()
+
+    spread_all().wait_send()
+    gather_all().wait_send()
+    pltpu.make_async_remote_copy(
+        outbox, near, s1, r1.at[0], device_id={"dp": sibling}, device_id_type=MESH
+    ).wait_send()
+    pltpu.make_async_remote_copy(
+        summed.at[pl.ds(0, pairs)], mid, s3, r3.at[0], device_id={"dp": across + core}, device_id_type=MESH
+    ).wait_send()
+    pltpu.make_async_remote_copy(
+        summed.at[pl.ds(0, pairs - 1)], far.at[pl.ds(0, pairs - 1)], s2, r2.at[0],
+        device_id={"dp": across + core}, device_id_type=MESH,
+    ).wait_send()
 
 
 def in_hbm(array):
@@ -446,8 +507,12 @@
             pltpu.VMEM(first.shape, f32),
             pltpu.VMEM(first.shape, f32),
             pltpu.VMEM(win.shape, bf16),
+            pltpu.VMEM((rank // 4, 128), bf16),
             pltpu.VMEM((rank, 128), bf16),
-            pltpu.VMEM((micro_count, tok_rows, rank), bf16),
+            pltpu.VMEM((rank, 128), bf16),
+            pltpu.VMEM((rows, rank), f32),
+            pltpu.VMEM((2, rows // 4, 2 * rank), bf16),
+            pltpu.VMEM((2, rows // 4, 2 * rank), bf16),
             pltpu.VMEM((micro_count, tok_rows, rank), bf16),
             pltpu.VMEM((micro_count, tok_rows, rank), bf16),
             pltpu.VMEM((n, 2, 2 * slab, 128), bf16),
@@ -460,10 +525,10 @@
             pltpu.VMEM((block_rows + pad, 128), f32),
             pltpu.VMEM((n, block_rows + pad, 128), bf16),
             group, group, group, fewer, fewer,
-            dma((3,)), dma((4,)), dma((chunks,)), dma((chunks,)),
-            dma((2,)), dma((2,)), dma((2,)), dma((2,)), dma((3,)), dma((3,)), dma, dma,
-            dma((n,)), dma((n,)), dma((n,)), dma((n,)), dma((2,)),
-            dma((n // 2,)), dma((n // 2,)), dma((n // 4,)), dma((n // 4,)), dma((n // 4,)), dma((n // 4,)),
+            dma((3,)), dma((4,)), dma((3,)), dma((3,)),
+            dma((3,)), dma((3,)), dma((2,)), dma((2,)), dma, dma, dma, dma, dma((2,)), dma((2,)),
+            dma, dma, dma, dma, dma((2,)),
+            dma, dma((n // 2,)), dma, dma((n // 4,)), dma, dma((n // 4,)),
         ],
         compiler_params=pltpu.CompilerParams(
             collective_id=0, has_side_effects=True, vmem_limit_bytes=44 * 1024 * 1024

time: 41.1 us -> 34.5 us (0.84)
  the two profiles are of different devices: /device:TPU:25 before, /device:TPU:0 now
where the time goes in v2:
time: 34.5 us; the launch traced here: 34 us
  Pallas kernels  33.3 us (97%)
  between operations  0.64 us (2%)
    pallas_call x1, Pallas kernels, relay(): pl.pallas_call(functools.partial(relay_kernel, n, block_rows, pad), out_s...  31.1 us
    pallas_call x1, Pallas kernels, finish(): pl.pallas_call(finish_kernel, out_shape=(jax.ShapeDtypeStruct((micro_coun...  2.24 us

profile of v2, /device:TPU:0, one launch (start us, length us, event | category | flops | bytes accessed | tf_op | source)
XLA Modules:
  0.0 34.0 jit_solution(14242199029971989273)
XLA Ops:
  0.6 31.1 %relay.1 = (bf16[384,5376]{1,0:T(8,128)(2,1)S(1)}, f32[336,128]{1,0:T(8,128)S(1)}, f32[336,128]{1,0:T(8,128)S(1)}, f32[336,128]{1,0:T(8,128)S(1)}) custom-call(s32[16]{0:T(128)} %bitcast.18, s32[8]{0:T(128)} %bitcast.19, s32[8]{0:T(128)} %plan_hbm.1, bf16[8,48,5376]{2,1,0:T(8,128)(2,1)} %bitcast.13, bf16[8,48,5376]{2,1,0:T(8,128)(2,1)} %l_hbm.1, ...), custom_call_target="tpu_custom_call" | custom-call | tf_op jit(solution)/shard_map/relay/pallas_call | solution.py:493
  31.7 2.2 %finish.1 = (bf16[8,48,5376]{2,1,0:T(8,128)(2,1)}, f32[336,128]{1,0:T(8,128)}, f32[336,128]{1,0:T(8,128)}, f32[336,128]{1,0:T(8,128)}) custom-call(bf16[384,5376]{1,0:T(8,128)(2,1)S(1)} %get-tuple-element.12.o_ref, f32[336,128]{1,0:T(8,128)S(1)} %get-tuple-element.13.total_ref, f32[336,128]{1,0:T(8,128)S(1)} %get-tuple-element.14.m_ref, ...), custom_call_target="tpu_custom_call" | custom-call | tf_op jit(solution)/shard_map/finish/pallas_call | solution.py:562

commit v3 on v2

--- a/solution.py
+++ b/solution.py
@@ -88,17 +88,20 @@
     weights = [
         started(src, dst, g_sem.at[k])
         for k, (src, dst) in enumerate(
-            ((m_hbm, m_buf), (v_hbm, v_buf), (win_hbm, win_buf), (wout_hbm, wout_buf))
+            ((win_hbm, win_buf), (wout_hbm, wout_buf), (m_hbm, m_buf), (v_hbm, v_buf))
         )
     ]
     micro_count, tok_rows, _ = x_buf.shape
     rows = micro_count * tok_rows
-    edges = [micro_count * k // 8 for k in (0, 4, 6, 8)]
+    edges = [micro_count * k // 8 for k in (0, 3, 6, 8)]
     spans = [pl.ds(a, b - a) for a, b in zip(edges, edges[1:])]
     loads = []
-    for g, span in enumerate(spans):
-        loads.append(started(x_hbm.at[span], x_buf.at[span], x_sem.at[g]))
-        loads.append(started(l_hbm.at[span], l_buf.at[span], l_sem.at[g]))
+
+    def load_tokens(g):
+        loads.append(started(x_hbm.at[spans[g]], x_buf.at[spans[g]], x_sem.at[g]))
+        loads.append(started(l_hbm.at[spans[g]], l_buf.at[spans[g]], l_sem.at[g]))
+
+    load_tokens(0)
 
     half, quarter = rank // 2, rank // 4
 
@@ -160,8 +163,9 @@
             p_out.at[k], p_got.at[k], p_send.at[k], p_recv.at[k], device_id={"section": other}, device_id_type=MESH
         )
 
-    def spread_copy(d):
-        peer = lax.rem(me + d, n)
+    def spread_copy(d, lane_at):
+        spot = lax.rem(pair * 2 + core + d, chips)
+        peer = spot // 2 * 4 + lane_at * 2 + lax.rem(spot, 2)
         return pltpu.make_async_remote_copy(
             pieces.at[peer], spread.at[me], a_send, a_recv,
             device_id={"dp": peer}, device_id_type=MESH,
@@ -191,35 +195,47 @@
             outbox.at[to], near.at[to], s1, r1.at[to], device_id={"dp": sibling}, device_id_type=MESH
         )
 
-    def mid_copy(at):
-        return pltpu.make_async_remote_copy(
-            summed.at[at * 2 + 1 - lane], mid.at[at], s3, r3.at[at],
+    side = pair // 2
+    inner = lax.rem(pair + side, 2)
+    beside = pair + 1 - 2 * lax.rem(pair, 2)
+    outward, inward = 3 * (1 - side), 2 - side
+    turns = [
+        jnp.where(inner == 1, there, here)
+        for there, here in ((beside, outward), (outward, inward), (inward, beside), (pair, pair))
+    ]
+    cut = (block_rows + pad) // 2
+    halves = (pl.ds(0, cut), pl.ds(cut, cut))
+
+    def mid_copy(at, h):
+        return pltpu.make_async_remote_copy(
+            summed.at[at * 2 + 1 - lane, halves[h]], mid.at[at, halves[h]], s3, r3.at[at * 2 + h],
             device_id={"dp": across + core}, device_id_type=MESH,
         )
 
-    def far_copy(d):
-        to = lax.rem(pair + d, pairs) * 2 + lane
-        return pltpu.make_async_remote_copy(
-            summed.at[to], far.at[d], s2, r2.at[d],
-            device_id={"dp": to * 2 + core}, device_id_type=MESH,
-        )
-
-    pl.semaphore_wait(barrier, n + 3)
-
-    @pl.when(section == 0)
-    def _():
-        lend(wout_hbm, high).start()
-
-    @pl.when(section == 1)
-    def _():
-        lend(win_hbm, low).start()
-
+    def far_copy(step, h):
+        at = turns[step]
+        slot = jnp.where(inner == 1, 2 if step == 0 else 3, step)
+        to = jnp.where(inner == 1, at, beside)
+        return pltpu.make_async_remote_copy(
+            summed.at[at * 2 + lane, halves[h]], far.at[slot, halves[h]], s2, r2.at[slot * 2 + h],
+            device_id={"dp": (to * 2 + lane) * 2 + core}, device_id_type=MESH,
+        )
+
+    def far_arrival(slot, h):
+        return pltpu.make_async_remote_copy(
+            summed.at[0, halves[h]], far.at[slot, halves[h]], s2, r2.at[slot * 2 + h],
+            device_id={"dp": (beside * 2 + lane) * 2 + core}, device_id_type=MESH,
+        )
 
     part = block_rows // n
     slab = pieces.shape[2] // 2
     filler = [jnp.zeros((slab - part, 128), jnp.float32)] if slab > part else []
     weights[0].wait()
     weights[1].wait()
+    load_tokens(1)
+    weights[2].wait()
+    weights[3].wait()
+    load_tokens(2)
     for t in range(n):
         for h in range(2):
             start = h * block_rows + t * part
@@ -227,9 +243,24 @@
                 [m_buf[start : start + part, :]] + filler + [v_buf[start : start + part, :]] + filler, axis=0
             ).astype(jnp.bfloat16)
 
-    @pl.loop(1, n)
+    pl.semaphore_wait(barrier, n + 3)
+
+    @pl.when(section == 0)
+    def _():
+        lend(wout_buf, high).start()
+
+    @pl.when(section == 1)
+    def _():
+        lend(win_buf, low).start()
+
+
+    @pl.loop(0, chips)
     def _(d):
-        spread_copy(d).start()
+        spread_copy(d, 1 - lane).start()
+
+    @pl.loop(1, chips)
+    def _(d):
+        spread_copy(d, lane).start()
 
     own = started(pieces.at[me], spread.at[me], own_sem.at[0])
     for load in ints:
@@ -247,8 +278,6 @@
     def tokens(ref, cols):
         return ref[:, :, cols].reshape(rows, -1)
 
-    weights[2].wait()
-    weights[3].wait()
     pres, acts, slopes = [], [], []
     sent = 0
     for g, span in enumerate(spans):
@@ -273,7 +302,7 @@
     hidden_t = jax.nn.silu(pre).T.astype(jnp.bfloat16)
     act_buf[...] = act
 
-    lend(win_hbm, low).wait_recv()
+    lend(win_buf, low).wait_recv()
 
     def mixed(weight, cols):
         value = nt_dot(w_ref[parts[0], low], weight[:, cols])
@@ -303,7 +332,13 @@
 
     @pl.when(section == 1)
     def _():
+        w_copy(2).start()
+        w_copy(1).start()
         p_up[...] = jnp.zeros_like(p_up)
+        blank = jnp.zeros((quarter, width), jnp.bfloat16)
+        w_ref[parts[0], high] = blank[:, : width - tiles // 2 * 128]
+        for spot in (parts[1], *their_parts):
+            w_ref[spot, :] = blank
 
     @pl.when(section == 0)
     def _():
@@ -328,8 +363,6 @@
             p_in, mix_t[:, :rank]
         )
 
-    w_copy(2).start()
-    w_copy(1).start()
     grad = act_buf[...] * slope
     p_now[...] = grad.astype(jnp.bfloat16).reshape(p_now.shape)
     p_t = grad.T.astype(jnp.bfloat16)
@@ -343,6 +376,21 @@
             odd = gin[pl.ds(start + 1, block_rows, stride=2), :]
             blocks[b, :block_rows, :] = jnp.concatenate([even, odd], axis=1).astype(jnp.bfloat16)
 
+    for lane_at in (1 - lane, lane):
+        for at in turns:
+            to = at * 2 + lane_at
+            outbox[to] = blocks[order[to * 2 + 1 - core]]
+            near_copy(to).start()
+
+    for at in turns:
+        to = at * 2 + 1 - lane
+        near_copy(to).wait_recv()
+        for h, part_of in enumerate(halves):
+            summed[to, part_of] = (
+                blocks[order[to * 2 + core], part_of].astype(jnp.float32) + near[to, part_of].astype(jnp.float32)
+            ).astype(jnp.bfloat16)
+            mid_copy(at, h).start()
+
     own.wait()
 
     spread_all().wait_recv()
@@ -356,39 +404,25 @@
         gather_copy(d).start()
 
     keep = started(chosen.at[me], got.at[me], own_sem.at[1])
-    table = [sorted(range(pairs), key=lambda at, p=p: (-abs(at - p), at)) for p in range(pairs)]
-    turns = [sum(jnp.where(pair == p, table[p][k], 0) for p in range(pairs)) for k in range(pairs)]
-    for side in (1 - lane, lane):
-        for at in turns:
-            to = at * 2 + side
-            outbox[to] = blocks[order[to * 2 + 1 - core]]
-            near_copy(to).start()
-
-    for at in turns:
-        to = at * 2 + 1 - lane
-        near_copy(to).wait_recv()
-        summed[to] = (
-            blocks[order[to * 2 + core]].astype(jnp.float32) + near[to].astype(jnp.float32)
-        ).astype(jnp.bfloat16)
-        mid_copy(at).start()
-
-    w_copy(2).wait_recv()
-    forward(0).start()
-    w_copy(1).wait_recv()
-    forward(1).start()
+
+    @pl.when(section == 0)
+    def _():
+        w_copy(2).wait_recv()
+        forward(0).start()
+        w_copy(1).wait_recv()
+        forward(1).start()
 
 
     def drained(ref, cols):
         return jnp.concatenate([ref[plan_ref[m], :, cols] for m in range(micro_count)], axis=0)
 
     p_up_turn, p_now_turn = drained(p_up, slice(None)), drained(p_now, slice(None))
-    forwarded(0).wait_recv()
-    forwarded(1).wait_recv()
 
     def emit(c):
         cols = pl.ds(c * cw, cw)
         incoming = (
-            drained(l_buf, cols).astype(jnp.float32) + jnp.dot(p_up_turn, w_ref[:, cols], preferred_element_type=jnp.float32)
+            drained(l_buf, cols).astype(jnp.float32)
+            + jnp.dot(p_up_turn, w_ref[:, cols], preferred_element_type=jnp.float32)
         ).astype(jnp.bfloat16)
         o_ref[:, cols] = (
             incoming.astype(jnp.float32)
@@ -397,24 +431,38 @@
 
     emitted = 0
     for step, at in enumerate(turns):
-        until = -(-chunks * (step + 1) // pairs)
+        to = at * 2 + lane
+        near_copy(to).wait_recv()
+        for h, part_of in enumerate(halves):
+            mid_copy(at, h).wait_recv()
+            joined = (
+                blocks[order[to * 2 + core], part_of].astype(jnp.float32)
+                + near[to, part_of].astype(jnp.float32)
+                + mid[at, part_of].astype(jnp.float32)
+            )
+            if step == pairs - 1:
+                acc[part_of, :] = joined
+                continue
+            summed[to, part_of] = joined.astype(jnp.bfloat16)
+            if step > 0:
+
+                @pl.when(inner == 1)
+                def _():
+                    far_arrival(step - 1, h).wait_recv()
+                    summed[to, part_of] = (joined + far[step - 1, part_of].astype(jnp.float32)).astype(jnp.bfloat16)
+
+            far_copy(step, h).start()
+        if step == 0:
+
+            @pl.when(section == 0)
+            def _():
+                forwarded(0).wait_recv()
+                forwarded(1).wait_recv()
+
+        until = (chunks * (step + 1) + pairs - 1) // pairs if step < pairs - 1 else chunks
         for c in range(emitted, until):
             emit(c)
         emitted = until
-        to = at * 2 + lane
-        near_copy(to).wait_recv()
-        mid_copy(at).wait_recv()
-        joined = (
-            blocks[order[to * 2 + core]].astype(jnp.float32)
-            + near[to].astype(jnp.float32)
-            + mid[at].astype(jnp.float32)
-        )
-
-        if step < pairs - 1:
-            summed[to] = joined.astype(jnp.bfloat16)
-            far_copy(lax.rem(at - pair + pairs, pairs)).start()
-        else:
-            acc[...] = joined
 
     keep.wait()
 
@@ -426,10 +474,10 @@
         first_ref[place, :] = held[:part, :]
         second_ref[place, :] = held[slab : slab + part, :]
 
-    @pl.loop(1, pairs)
-    def _(d):
-        far_copy(d).wait_recv()
-        acc[...] += far[d].astype(jnp.float32)
+    for slot in (2, 3):
+        for h, part_of in enumerate(halves):
+            far_arrival(slot, h).wait_recv()
+            acc[part_of, :] += far[slot, part_of].astype(jnp.float32)
 
     shared = acc[block_rows : block_rows + lines, :rank].astype(jnp.bfloat16)
     for c in range(chunks):
@@ -438,13 +486,12 @@
             turn[pl.ds(c * (cw // 128) + t, lines, stride=tiles), :] = fix[:, t * 128 : (t + 1) * 128]
     total_ref[...] = acc[:block_rows, :] + turn[...]
 
-    lend(win_hbm, low).wait_send()
-    for k in range(2):
-        w_copy(k + 1).wait_send()
-        forward(k).wait_send()
+    lend(win_buf, low).wait_send()
 
     @pl.when(section == 0)
     def _():
+        forward(0).wait_send()
+        forward(1).wait_send()
         pltpu.make_async_remote_copy(
             mix.at[pl.ds(0, 3 * quarter)], mix.at[pl.ds(0, 3 * quarter)], k_send, k_recv,
             device_id={"dp": sibling}, device_id_type=MESH,
@@ -452,6 +499,8 @@
 
     @pl.when(section == 1)
     def _():
+        w_copy(1).wait_send()
+        w_copy(2).wait_send()
         p_copy(0).wait_send()
         p_copy(1).wait_send()
         pltpu.make_async_remote_copy(
@@ -467,7 +516,7 @@
         summed.at[pl.ds(0, pairs)], mid, s3, r3.at[0], device_id={"dp": across + core}, device_id_type=MESH
     ).wait_send()
     pltpu.make_async_remote_copy(
-        summed.at[pl.ds(0, pairs - 1)], far.at[pl.ds(0, pairs - 1)], s2, r2.at[0],
+        summed.at[pl.ds(0, 3)], far.at[pl.ds(0, 3)], s2, r2.at[0],
         device_id={"dp": across + core}, device_id_type=MESH,
     ).wait_send()
 
@@ -528,7 +577,7 @@
             dma((3,)), dma((4,)), dma((3,)), dma((3,)),
             dma((3,)), dma((3,)), dma((2,)), dma((2,)), dma, dma, dma, dma, dma((2,)), dma((2,)),
             dma, dma, dma, dma, dma((2,)),
-            dma, dma((n // 2,)), dma, dma((n // 4,)), dma, dma((n // 4,)),
+            dma, dma((n // 2,)), dma, dma((8,)), dma, dma((n // 2,)),
         ],
         compiler_params=pltpu.CompilerParams(
             collective_id=0, has_side_effects=True, vmem_limit_bytes=44 * 1024 * 1024
@@ -736,7 +785,7 @@
     )
     place_of_block = owners_new % 2 * (replicas // 2) + owners_new // 2
     lines = (block_len // 128, 128)
-    if sections == 2 and replicas % 4 == 0 and block_len % (128 * replicas) == 0:
+    if sections == 2 and replicas == 16 and block_len % (128 * replicas) == 0:
         turned_in = weight_in.T
         row_lines = (2 * block_len // 128, 128)
         o, total, first_old, second_old = relay(

time: 34.5 us -> 32 us (0.928); the launches traced: 34 us -> 31.9 us
  Pallas kernels: 33.3 us -> 31.3 us
    pallas_call x1, Pallas kernels: 31.1 us -> 29 us  [relay(): pl.pallas_call(functools.partial(relay_kernel, n, block_rows, pad), out_s...]
where the time goes in v3:
time: 32 us; the launch traced here: 31.9 us
  Pallas kernels  31.3 us (98%)
  between operations  0.64 us (2%)
    pallas_call x1, Pallas kernels, relay(): pl.pallas_call(functools.partial(relay_kernel, n, block_rows, pad), out_s...  29 us
    pallas_call x1, Pallas kernels, finish(): pl.pallas_call(finish_kernel, out_shape=(jax.ShapeDtypeStruct((micro_coun...  2.24 us

profile of v3, /device:TPU:0, one launch (start us, length us, event | category | flops | bytes accessed | tf_op | source)
XLA Modules:
  0.0 31.9 jit_solution(17933597756975636327)
XLA Ops:
  0.6 29.0 %relay.1 = (bf16[384,5376]{1,0:T(8,128)(2,1)S(1)}, f32[336,128]{1,0:T(8,128)S(1)}, f32[336,128]{1,0:T(8,128)S(1)}, f32[336,128]{1,0:T(8,128)S(1)}) custom-call(s32[16]{0:T(128)} %bitcast.18, s32[8]{0:T(128)} %bitcast.19, s32[8]{0:T(128)} %plan_hbm.1, bf16[8,48,5376]{2,1,0:T(8,128)(2,1)} %bitcast.13, bf16[8,48,5376]{2,1,0:T(8,128)(2,1)} %l_hbm.1, ...), custom_call_target="tpu_custom_call" | custom-call | tf_op jit(solution)/shard_map/relay/pallas_call | solution.py:542
  29.7 2.2 %finish.1 = (bf16[8,48,5376]{2,1,0:T(8,128)(2,1)}, f32[336,128]{1,0:T(8,128)}, f32[336,128]{1,0:T(8,128)}, f32[336,128]{1,0:T(8,128)}) custom-call(bf16[384,5376]{1,0:T(8,128)(2,1)S(1)} %get-tuple-element.12.o_ref, f32[336,128]{1,0:T(8,128)S(1)} %get-tuple-element.13.total_ref, f32[336,128]{1,0:T(8,128)S(1)} %get-tuple-element.14.m_ref, ...), custom_call_target="tpu_custom_call" | custom-call | tf_op jit(solution)/shard_map/finish/pallas_call | solution.py:611
